TPU v7x, 8 devices: a whole 2x2x1 slice. The times are simulated.
8 devices in a mesh: dp: 1 (over z), fsdp: 8 (over y, x, core).
Axes of the slice: x: 2, y: 2, z: 1, core: 2. Of those that a mesh axis runs over, the one named last changes fastest.
Arguments:
- tokens: bfloat16 [16, 512, 7168], P(('dp', 'fsdp'))
- gain_in: bfloat16 [7168], P('fsdp')
- w_dq: bfloat16 [7168, 1536], P('fsdp')
- gain_q: bfloat16 [1536], P('fsdp')
- w_uq: bfloat16 [1536, 12288], P('fsdp')
- w_dkv: bfloat16 [7168, 576], P('fsdp')
- gain_kv: bfloat16 [512], P('fsdp')
- w_ukv: bfloat16 [512, 16384], P('fsdp')
- w_out: bfloat16 [8192, 7168], P('fsdp')
Outputs:
- output 1: bfloat16 [16, 512, 7168], P(('dp', 'fsdp'))
- output 2: bfloat16 [16, 512, 512], P(('dp', 'fsdp'))
- output 3: bfloat16 [16, 512, 64], P(('dp', 'fsdp'))
All inputs are finite; a program needn't handle non-finite values.
Results may differ from a plain program's by a relative error of at most 0.00556248.
Values are sent between devices in bfloat16 or wider.
A program may use at most 1 GiB of HBM per device.

v0:
```python
import jax
import jax.numpy as jnp
from jax import lax
from jax.sharding import PartitionSpec as P, NamedSharding

EPSILON = 1e-6
ROPE_THETA = 10000.0


def rms_scale(values_in, gain_vec):
    values_f32 = values_in.astype(jnp.float32)
    inv_rms = lax.rsqrt(jnp.mean(values_f32 * values_f32, axis=-1, keepdims=True) + EPSILON)
    return values_f32 * inv_rms * gain_vec.astype(jnp.float32)


def rope_tables(seq_len, rope_dim):
    half_dim = rope_dim // 2
    inv_freq = ROPE_THETA ** (-2.0 * jnp.arange(half_dim, dtype=jnp.float32) / rope_dim)
    angles = jnp.arange(seq_len, dtype=jnp.float32)[:, None] * inv_freq[None, :]
    return jnp.cos(angles), jnp.sin(angles)


def apply_rope(values_in, cos_t, sin_t):
    half_dim = values_in.shape[-1] // 2
    lo_half = values_in[..., :half_dim]
    hi_half = values_in[..., half_dim:]
    return jnp.concatenate([lo_half * cos_t - hi_half * sin_t, hi_half * cos_t + lo_half * sin_t], axis=-1)


def head_dims(w_uq, w_dkv, gain_kv, w_ukv, w_out):
    rope_dim = w_dkv.shape[1] - gain_kv.shape[0]
    nope_total = w_ukv.shape[1] - w_out.shape[0]
    n_heads = (w_uq.shape[1] - nope_total) // rope_dim
    return n_heads, nope_total // n_heads, rope_dim, w_out.shape[0] // n_heads


def latents(tokens, gain_in, w_dq, gain_q, w_dkv, gain_kv, cos_t, sin_t):
    kv_rank = gain_kv.shape[0]
    normed = rms_scale(tokens, gain_in).astype(jnp.bfloat16)
    q_down = jnp.einsum('btd,dr->btr', normed, w_dq, preferred_element_type=jnp.float32)
    q_lat = rms_scale(q_down, gain_q).astype(jnp.bfloat16)
    kv_down = jnp.einsum('btd,dr->btr', normed, w_dkv, preferred_element_type=jnp.float32)
    latent = rms_scale(kv_down[:, :, :kv_rank], gain_kv).astype(jnp.bfloat16)
    k_pe = apply_rope(kv_down[:, :, kv_rank:], cos_t, sin_t).astype(jnp.bfloat16)
    return q_lat, latent, k_pe


def attend(q_lat, latent, k_pe, w_uq, w_ukv, w_out, head_info, cos_t, sin_t):
    n_heads, nope_dim, rope_dim, v_dim = head_info
    n_prompts = q_lat.shape[0]
    seq_len = q_lat.shape[1]
    q_full = jnp.einsum('btr,rc->btc', q_lat, w_uq, preferred_element_type=jnp.float32)
    q_full = q_full.reshape(n_prompts, seq_len, n_heads, nope_dim + rope_dim)
    q_nope = q_full[..., :nope_dim].astype(jnp.bfloat16)
    q_pe = apply_rope(q_full[..., nope_dim:], cos_t[:, None, :], sin_t[:, None, :]).astype(jnp.bfloat16)
    kv_up = jnp.einsum('btr,rc->btc', latent, w_ukv, preferred_element_type=jnp.float32).astype(jnp.bfloat16)
    kv_up = kv_up.reshape(n_prompts, seq_len, n_heads, nope_dim + v_dim)
    k_nope = kv_up[..., :nope_dim]
    values = kv_up[..., nope_dim:]
    score_scale = (nope_dim + rope_dim) ** -0.5
    scores = jnp.einsum('bqhd,bkhd->bhqk', q_nope, k_nope, preferred_element_type=jnp.float32)
    scores = scores + jnp.einsum('crie,cle->cirl', q_pe, k_pe, preferred_element_type=jnp.float32)
    causal = jnp.arange(seq_len)[:, None] >= jnp.arange(seq_len)[None, :]
    scores = jnp.where(causal, scores * score_scale, -1e30)
    attn_probs = jax.nn.softmax(scores, axis=-1).astype(jnp.bfloat16)
    attn_out = jnp.einsum('bhqk,bkhd->bqhd', attn_probs, values, preferred_element_type=jnp.float32).astype(jnp.bfloat16)
    attn_out = attn_out.reshape(n_prompts, seq_len, n_heads * v_dim)
    return jnp.einsum('btc,cd->btd', attn_out, w_out, preferred_element_type=jnp.float32)


def attend_each(q_lat, latent, k_pe, w_uq, w_ukv, w_out, head_info, cos_t, sin_t):
    def one_prompt(operands):
        q_one, lat_one, pe_one = operands
        return attend(q_one[None], lat_one[None], pe_one[None], w_uq, w_ukv, w_out, head_info, cos_t, sin_t)[0]

    return lax.map(one_prompt, (q_lat, latent, k_pe))


def solution(mesh):
    batch_spec = P(('dp', 'fsdp'))
    row_spec = P('fsdp')
    mat_spec = P('fsdp', None)

    def run_block(tokens, gain_in, w_dq, gain_q, w_uq, w_dkv, gain_kv, w_ukv, w_out):
        head_info = head_dims(w_uq, w_dkv, gain_kv, w_ukv, w_out)
        seq_len = tokens.shape[1]

        def local_block(tok_blk, gain_in_s, w_dq_s, gain_q_s, w_uq_s, w_dkv_s, gain_kv_s, w_ukv_s, w_out_s):
            cos_t, sin_t = rope_tables(seq_len, head_info[2])
            gain_in_all = lax.all_gather(gain_in_s, 'fsdp', tiled=True)
            w_dq_all = lax.all_gather(w_dq_s, 'fsdp', tiled=True)
            gain_q_all = lax.all_gather(gain_q_s, 'fsdp', tiled=True)
            w_dkv_all = lax.all_gather(w_dkv_s, 'fsdp', tiled=True)
            gain_kv_all = lax.all_gather(gain_kv_s, 'fsdp', tiled=True)
            q_lat, latent, k_pe = latents(tok_blk, gain_in_all, w_dq_all, gain_q_all, w_dkv_all, gain_kv_all, cos_t, sin_t)
            w_uq_all = lax.all_gather(w_uq_s, 'fsdp', tiled=True)
            w_ukv_all = lax.all_gather(w_ukv_s, 'fsdp', tiled=True)
            w_out_all = lax.all_gather(w_out_s, 'fsdp', tiled=True)
            proj_out = attend_each(q_lat, latent, k_pe, w_uq_all, w_ukv_all, w_out_all, head_info, cos_t, sin_t)
            y_blk = (tok_blk.astype(jnp.float32) + proj_out).astype(jnp.bfloat16)
            return y_blk, latent, k_pe

        mapped = jax.shard_map(
            local_block,
            mesh=mesh,
            in_specs=(batch_spec, row_spec, mat_spec, row_spec, mat_spec, mat_spec, row_spec, mat_spec, mat_spec),
            out_specs=(batch_spec, batch_spec, batch_spec),
            check_vma=False,
        )
        return mapped(tokens, gain_in, w_dq, gain_q, w_uq, w_dkv, gain_kv, w_ukv, w_out)

    return run_block
```

profile of v0, /device:TPU:0, one launch (start us, length us, event | category | flops | bytes accessed | tf_op | source)
XLA Modules:
  0.0 1551.6 jit_solution(6973721061095489184)
XLA Ops:
  11.1 25.6 %all-reduce.2 = (bf16[512]{0:T(512)(128)(2,1)S(1)}, bf16[1536]{0:T(1024)(128)(2,1)S(1)}) all-reduce(bf16[512]{0:T(512)(128)(2,1)S(1)} %dynamic-update-slice, bf16[1536]{0:T(1024)(128)(2,1)S(1)} %dynamic-update-slice.1), channel_id=1, replica_groups=mesh['dp'=1,'fsdp'=8] {'fsdp'}, use_global_device_ids=true, to_apply=%add | all-reduce | flops 2048 | bytes 8192
  36.8 12.4 all-gather
  49.3 8.1 fusion.35
  61.5 14.8 fusion.42
  78.1 91.7 %all-gather.11.cloned.1.call-done = bf16[7168,1536]{1,0:T(8,128)(2,1)} async-done(((bf16[896,1536]{1,0:T(8,128)(2,1)}), bf16[7168,1536]{1,0:T(8,128)(2,1)}) %all-gather.11.cloned.1.call-update) | async-done | bytes 22020112 | tf_op jit(solution)/shard_map/all_gather | solution.py:91
  169.8 28.0 %multiply_reduce_fusion = (f32[2,512]{1,0:T(2,128)S(1)}, f32[2,512,1536]{2,1,0:T(8,128)S(1)}) fusion(bf16[7168,1536]{1,0:T(8,128)(2,1)} %all-gather.11.cloned.1.call-done, bf16[2,512,7168]{2,1,0:T(8,128)(2,1)} %param.11, f32[7168]{0:T(1024)} %bitcast.116, f32[2,512]{1,0:T(2,128)} %copy-done.6), kind=kOutput, calls=%fused_computation.52 | convolution fusion | flops 22581084160 | bytes 43028480 | tf_op jit(solution)/shard_map/btd,dr->btr/dot_general | solution.py:40
  200.1 145.6 %all-gather.13.cloned.1.call-done = bf16[1536,12288]{1,0:T(8,128)(2,1)} async-done(((bf16[192,12288]{1,0:T(8,128)(2,1)}), bf16[1536,12288]{1,0:T(8,128)(2,1)}) %all-gather.13.cloned.1.call-update) | async-done | bytes 37748752 | tf_op jit(solution)/shard_map/all_gather | solution.py:96
  345.6 48.7 %copy.24 = bf16[1536,12288]{0,1:T(8,128)(2,1)} copy(bf16[1536,12288]{1,0:T(8,128)(2,1)} %all-gather.13.cloned.1.call-done) | data formatting | bytes 75497472
  394.3 37.1 %all-gather.9.cloned.1.call-done = bf16[512,16384]{1,0:T(8,128)(2,1)} async-done(((bf16[64,16384]{1,0:T(8,128)(2,1)}), bf16[512,16384]{1,0:T(8,128)(2,1)}) %all-gather.9.cloned.1.call-update) | async-done | bytes 16777232 | tf_op jit(solution)/shard_map/all_gather | solution.py:97
  431.4 512.3 %all-gather.15.cloned.1.call-done = bf16[8192,7168]{1,0:T(8,128)(2,1)} async-done(((bf16[1024,7168]{1,0:T(8,128)(2,1)}), bf16[8192,7168]{1,0:T(8,128)(2,1)}) %all-gather.15.cloned.1.call-update) | async-done | bytes 117440528 | tf_op jit(solution)/shard_map/all_gather | solution.py:98
  943.7 580.2 %while.13 = (s32[]{:T(128)}, f32[2,512,7168]{2,1,0:T(8,128)}, bf16[2,512,512]{2,1,0:T(8,128)(2,1)}, bf16[512,16384]{1,0:T(8,128)(2,1)}, bf16[2,512,1536]{2,1,0:T...) while((s32[]{:T(128)}, f32[2,512,7168]{2,1,0:T(8,128)}, ...), condition=%wide.region_6.7_spmd.clone.clone.clone, body=%wide.region_3.6_spmd.clone.clone.clone.sunk | while | flops 98964815872 | bytes 711394496 | solution.py:76
  963.5 15.8 %convolution_convert_fusion.2 = bf16[512,16384]{1,0:T(8,128)(2,1)} fusion(bf16[512,16384]{1,0:T(8,128)(2,1)} %get-tuple-element.289, bf16[2,512,512]{2,1,0:T(8,128)(2,1)} %get-tuple-element.288, s32[]{:T(128)S(6)} %copy.47), kind=kOutput, calls=%fused_computation.10.clone.1 | convolution fusion | flops 8598323200 | bytes 34078724 | tf_op jit(solution)/shard_map/while/body/eval_jaxpr/btr,rc->btc/dot_general | solution.py:56
  979.3 10.3 copy.40
  989.6 7.4 fusion.83
  997.0 12.9 copy.41
  1009.9 29.5 %convolution_bitcast_fusion.2 = f32[1,512,64,192]{1,3,2,0:T(8,128)} fusion(bf16[64,192,1536]{2,1,0:T(8,128)(2,1)} %bitcast.114, bf16[2,512,1536]{2,1,0:T(8,128)(2,1)} %get-tuple-element.290, s32[]{:T(128)S(6)} %copy.47), kind=kOutput, calls=%fused_computation.13.clone.1 | convolution fusion | flops 19327352832 | bytes 64487428 | tf_op jit(solution)/shard_map/while/body/eval_jaxpr/btr,rc->btc/dot_general | solution.py:52
  1044.3 23.7 %fusion.82 = f32[512,512,64]{1,0,2:T(8,128)} fusion(bf16[512,64,32]{0,2,1:T(8,128)(2,1)S(1)} %get-tuple-element.260, bf16[512,64,32]{0,2,1:T(8,128)(2,1)S(1)} %get-tuple-element.261, bf16[2,512,64]{1,2,0:T(8,128)(2,1)S(1)} %get-tuple-element.292, s32[]{:T(128)S(6)} %copy.47), kind=kOutput, calls=%fused_computation.18.clone.1 | convolution fusion | flops 2155872256 | bytes 71368704 | tf_op jit(solution)/shard_map/while/body/eval_jaxpr/crie,cle->cirl/dot_general | solution.py:62
  1068.0 53.4 %fusion.84 = (f32[64,512]{1,0:T(8,128)S(1)}, f32[1,64,512,512]{2,3,1,0:T(8,128)}) fusion(f32[512,512,64]{1,0,2:T(8,128)} %fusion.82, f32[1,512,64,192]{1,3,2,0:T(8,128)} %convolution_bitcast_fusion.2, bf16[1,512,64,128]{3,2,1,0:T(8,128)(2,1)} %get-tuple-element.262, pred[512,512]{0,1:T(8,128)(4,1)S(1)} %iota_compare_fusion.2), kind=kOutput, calls=%fused_computation.66.clone.2 | convolution fusion | flops 4362043392 | bytes 151388160 | tf_op jit(solution)/shard_map/while/body/eval_jaxpr/bqhd,bkhd->bhqk/dot_general | solution.py:61
  1121.4 21.0 %fusion.85 = f32[64,512]{1,0:T(8,128)S(1)} fusion(f32[1,64,512,512]{2,3,1,0:T(8,128)} %get-tuple-element.263, f32[64,512]{1,0:T(8,128)S(1)} %get-tuple-element.264), kind=kLoop, calls=%fused_computation.7.clone.1 | loop fusion | flops 33521664 | bytes 67371008 | tf_op jit(solution)/shard_map/while/body/eval_jaxpr/reduce_sum | solution.py:65
  1142.5 29.6 %fusion.86 = bf16[64,128,512]{2,1,0:T(8,128)(2,1)} fusion(f32[64,512]{1,0:T(8,128)S(1)} %fusion.85, f32[1,64,512,512]{2,3,1,0:T(8,128)} %get-tuple-element.263, f32[64,512]{1,0:T(8,128)S(1)} %get-tuple-element.264, bf16[1,512,64,128]{1,3,2,0:T(8,128)(2,1)} %copy.41), kind=kOutput, calls=%fused_computation.17.clone.1 | convolution fusion | flops 4349493248 | bytes 84148224 | tf_op jit(solution)/shard_map/while/body/eval_jaxpr/bhqk,bkhd->bqhd/dot_general | solution.py:66
  1172.0 71.5 %bitcast_dynamic-update-slice_fusion.2 = f32[2,512,7168]{2,1,0:T(8,128)} fusion(f32[2,512,7168]{2,1,0:T(8,128)} %get-tuple-element.277, s32[]{:T(128)S(6)} %copy.47, bf16[512,8192]{0,1:T(8,128)(2,1)} %bitcast.117, bf16[8192,7168]{1,0:T(8,128)(2,1)} %get-tuple-element.293), kind=kOutput, calls=%fused_computation.12.clone.1 | convolution fusion | flops 60129542144 | bytes 140509184 | tf_op jit(solution)/shard_map/while/body/eval_jaxpr/btc,cd->btd/dot_general | solution.py:68
  1243.9 15.8 %convolution_convert_fusion.2 = bf16[512,16384]{1,0:T(8,128)(2,1)} fusion(bf16[512,16384]{1,0:T(8,128)(2,1)} %get-tuple-element.289, bf16[2,512,512]{2,1,0:T(8,128)(2,1)} %get-tuple-element.288, s32[]{:T(128)S(6)} %copy.47), kind=kOutput, calls=%fused_computation.10.clone.1 | convolution fusion | flops 8598323200 | bytes 34078724 | tf_op jit(solution)/shard_map/while/body/eval_jaxpr/btr,rc->btc/dot_general | solution.py:56
  1259.7 10.3 copy.40
  1270.0 7.4 fusion.83
  1277.4 12.9 copy.41
  1290.3 29.5 %convolution_bitcast_fusion.2 = f32[1,512,64,192]{1,3,2,0:T(8,128)} fusion(bf16[64,192,1536]{2,1,0:T(8,128)(2,1)} %bitcast.114, bf16[2,512,1536]{2,1,0:T(8,128)(2,1)} %get-tuple-element.290, s32[]{:T(128)S(6)} %copy.47), kind=kOutput, calls=%fused_computation.13.clone.1 | convolution fusion | flops 19327352832 | bytes 64487428 | tf_op jit(solution)/shard_map/while/body/eval_jaxpr/btr,rc->btc/dot_general | solution.py:52
  1324.7 23.7 %fusion.82 = f32[512,512,64]{1,0,2:T(8,128)} fusion(bf16[512,64,32]{0,2,1:T(8,128)(2,1)S(1)} %get-tuple-element.260, bf16[512,64,32]{0,2,1:T(8,128)(2,1)S(1)} %get-tuple-element.261, bf16[2,512,64]{1,2,0:T(8,128)(2,1)S(1)} %get-tuple-element.292, s32[]{:T(128)S(6)} %copy.47), kind=kOutput, calls=%fused_computation.18.clone.1 | convolution fusion | flops 2155872256 | bytes 71368704 | tf_op jit(solution)/shard_map/while/body/eval_jaxpr/crie,cle->cirl/dot_general | solution.py:62
  1348.5 53.4 %fusion.84 = (f32[64,512]{1,0:T(8,128)S(1)}, f32[1,64,512,512]{2,3,1,0:T(8,128)}) fusion(f32[512,512,64]{1,0,2:T(8,128)} %fusion.82, f32[1,512,64,192]{1,3,2,0:T(8,128)} %convolution_bitcast_fusion.2, bf16[1,512,64,128]{3,2,1,0:T(8,128)(2,1)} %get-tuple-element.262, pred[512,512]{0,1:T(8,128)(4,1)S(1)} %iota_compare_fusion.2), kind=kOutput, calls=%fused_computation.66.clone.2 | convolution fusion | flops 4362043392 | bytes 151388160 | tf_op jit(solution)/shard_map/while/body/eval_jaxpr/bqhd,bkhd->bhqk/dot_general | solution.py:61
  1401.9 21.0 %fusion.85 = f32[64,512]{1,0:T(8,128)S(1)} fusion(f32[1,64,512,512]{2,3,1,0:T(8,128)} %get-tuple-element.263, f32[64,512]{1,0:T(8,128)S(1)} %get-tuple-element.264), kind=kLoop, calls=%fused_computation.7.clone.1 | loop fusion | flops 33521664 | bytes 67371008 | tf_op jit(solution)/shard_map/while/body/eval_jaxpr/reduce_sum | solution.py:65
  1422.9 29.5 %fusion.86 = bf16[64,128,512]{2,1,0:T(8,128)(2,1)} fusion(f32[64,512]{1,0:T(8,128)S(1)} %fusion.85, f32[1,64,512,512]{2,3,1,0:T(8,128)} %get-tuple-element.263, f32[64,512]{1,0:T(8,128)S(1)} %get-tuple-element.264, bf16[1,512,64,128]{1,3,2,0:T(8,128)(2,1)} %copy.41), kind=kOutput, calls=%fused_computation.17.clone.1 | convolution fusion | flops 4349493248 | bytes 84148224 | tf_op jit(solution)/shard_map/while/body/eval_jaxpr/bhqk,bkhd->bqhd/dot_general | solution.py:66
  1452.5 71.4 %bitcast_dynamic-update-slice_fusion.2 = f32[2,512,7168]{2,1,0:T(8,128)} fusion(f32[2,512,7168]{2,1,0:T(8,128)} %get-tuple-element.277, s32[]{:T(128)S(6)} %copy.47, bf16[512,8192]{0,1:T(8,128)(2,1)} %bitcast.117, bf16[8192,7168]{1,0:T(8,128)(2,1)} %get-tuple-element.293), kind=kOutput, calls=%fused_computation.12.clone.1 | convolution fusion | flops 60129542144 | bytes 140509184 | tf_op jit(solution)/shard_map/while/body/eval_jaxpr/btc,cd->btd/dot_general | solution.py:68
  1523.9 21.0 %fusion.38 = bf16[2,512,7168]{2,1,0:T(8,128)(2,1)} fusion(f32[2,512,7168]{2,1,0:T(8,128)} %get-tuple-element.61, bf16[2,512,7168]{2,1,0:T(8,128)(2,1)} %param.11), kind=kLoop, calls=%fused_computation.46 | loop fusion | flops 22020096 | bytes 58720256 | tf_op jit(solution)/shard_map/convert_element_type | solution.py:100
  (65 shorter events, 22.7 us)
Async XLA Ops:
  7.2 3.4 copy-start.7
  7.2 3.5 copy-start.8
  7.2 3.7 copy-start.9
  7.2 54.3 %all-gather.7.cloned.1.call-start = ((), (), s32[]{:S(2)}) async-start(), calls=%async_computation | async-start | bytes 9289728 | tf_op jit(solution)/shard_map/all_gather | solution.py:93
  7.9 161.8 %all-gather.11.cloned.1.call-start = ((), (), s32[]{:S(2)}) async-start(), calls=%async_computation.2 | async-start | bytes 24772608 | tf_op jit(solution)/shard_map/all_gather | solution.py:91
  8.7 337.0 %all-gather.13.cloned.1.call-start = ((), (), s32[]{:S(2)}) async-start(), calls=%async_computation.3 | async-start | bytes 42467328 | tf_op jit(solution)/shard_map/all_gather | solution.py:96
  9.4 422.0 %all-gather.9.cloned.1.call-start = ((), (), s32[]{:S(2)}) async-start(), calls=%async_computation.1 | async-start | bytes 18874368 | tf_op jit(solution)/shard_map/all_gather | solution.py:97
  10.0 933.8 %all-gather.15.cloned.1.call-start = ((), (), s32[]{:S(2)}) async-start(), calls=%async_computation.4 | async-start | bytes 132120576 | tf_op jit(solution)/shard_map/all_gather | solution.py:98
  49.2 27.0 %copy-start.3 = (f32[8,1,896]{2,1,0:T(1,128)}, f32[8,1,896]{2,1,0:T(1,128)S(1)}, u32[]{:S(2)}) copy-start(f32[8,1,896]{2,1,0:T(1,128)S(1)} %convert_element_type.60) | copy-start | bytes 86020
  57.4 18.9 %copy-start.6 = (f32[2,512]{1,0:T(2,128)}, f32[2,512]{1,0:T(2,128)S(1)}, u32[]{:S(2)}) copy-start(f32[2,512]{1,0:T(2,128)S(1)} %add_rsqrt_fusion.2) | copy-start | bytes 12292
  963.1 16.2 %copy-start.4 = (f32[32]{0:T(128)}, f32[32]{0:T(128)S(1)}, u32[]{:S(2)}) copy-start(f32[32]{0:T(128)S(1)} %get-tuple-element.294) | copy-start | bytes 388 | tf_op jit(solution)/shard_map/while
  963.1 81.2 %copy-start = (bf16[2,512,64]{1,2,0:T(8,128)(2,1)}, bf16[2,512,64]{1,2,0:T(8,128)(2,1)S(1)}, u32[]{:S(2)}) copy-start(bf16[2,512,64]{1,2,0:T(8,128)(2,1)S(1)} %get-tuple-element.292) | copy-start | bytes 393220 | tf_op jit(solution)/shard_map/while
  1172.0 71.5 %copy-start.1 = (bf16[2,512,64]{1,2,0:T(8,128)(2,1)S(1)}, bf16[2,512,64]{1,2,0:T(8,128)(2,1)}, u32[]{:S(2)}) copy-start(bf16[2,512,64]{1,2,0:T(8,128)(2,1)} %copy-done) | copy-start | bytes 393220 | tf_op jit(solution)/shard_map/while
  1172.0 71.5 %copy-start.5 = (f32[32]{0:T(128)S(1)}, f32[32]{0:T(128)}, u32[]{:S(2)}) copy-start(f32[32]{0:T(128)} %copy-done.4) | copy-start | bytes 388 | tf_op jit(solution)/shard_map/while
  1243.5 16.2 %copy-start.4 = (f32[32]{0:T(128)}, f32[32]{0:T(128)S(1)}, u32[]{:S(2)}) copy-start(f32[32]{0:T(128)S(1)} %get-tuple-element.294) | copy-start | bytes 388 | tf_op jit(solution)/shard_map/while
  1243.5 81.2 %copy-start = (bf16[2,512,64]{1,2,0:T(8,128)(2,1)}, bf16[2,512,64]{1,2,0:T(8,128)(2,1)S(1)}, u32[]{:S(2)}) copy-start(bf16[2,512,64]{1,2,0:T(8,128)(2,1)S(1)} %get-tuple-element.292) | copy-start | bytes 393220 | tf_op jit(solution)/shard_map/while
  1452.5 71.4 %copy-start.1 = (bf16[2,512,64]{1,2,0:T(8,128)(2,1)S(1)}, bf16[2,512,64]{1,2,0:T(8,128)(2,1)}, u32[]{:S(2)}) copy-start(bf16[2,512,64]{1,2,0:T(8,128)(2,1)} %copy-done) | copy-start | bytes 393220 | tf_op jit(solution)/shard_map/while
  1452.5 71.4 %copy-start.5 = (f32[32]{0:T(128)S(1)}, f32[32]{0:T(128)}, u32[]{:S(2)}) copy-start(f32[32]{0:T(128)} %copy-done.4) | copy-start | bytes 388 | tf_op jit(solution)/shard_map/while
  1523.9 21.0 %copy-start.2 = (bf16[2,512,64]{1,2,0:T(8,128)(2,1)}, bf16[2,512,64]{1,2,0:T(8,128)(2,1)S(1)}, u32[]{:S(2)}) copy-start(bf16[2,512,64]{1,2,0:T(8,128)(2,1)S(1)} %get-tuple-element.310) | copy-start | bytes 393220
Sparse Core Ops, SparseCore 0:
  9.8 51.5 all-gather.6
  63.3 106.4 all-gather.10
  171.6 173.9 all-gather.12
  347.3 84.0 all-gather.8
  433.1 510.5 all-gather.14
where the time goes:
time: 1560 us; the launch traced here: 1550 us
  waiting for transfers between devices  794 us (51%)
  matrix products  490 us (31%)
  local copies, waits for them, and re-layouts  112 us (7%)
  other arithmetic  84.9 us (5%)
  blocking collectives  38.1 us (2%)
  loops' own time  19.4 us (1%)
    all_gather x1, waiting for transfers between devices, local_block(): w_out_all = lax.all_gather(w_out_s, 'fsdp', tiled=True)  512 us
    all_gather x1, waiting for transfers between devices, local_block(): w_uq_all = lax.all_gather(w_uq_s, 'fsdp', tiled=True)  146 us
    dot_general x2, matrix products, attend(): jnp.einsum('btc,cd->btd', attn_out, w_out, preferred_element_type=jnp.flo...  143 us
    dot_general x2, matrix products, attend(): jnp.einsum('bqhd,bkhd->bhqk', q_nope, k_nope, preferred_element_type=jnp....  107 us
    all_gather x1, waiting for transfers between devices, local_block(): w_dq_all = lax.all_gather(w_dq_s, 'fsdp', tiled=True)  91.7 us
    dot_general x2, matrix products, attend(): jnp.einsum('bhqk,bkhd->bqhd', attn_probs, values, preferred_element_type=...  59.1 us
    dot_general x2, matrix products, attend(): jnp.einsum('btr,rc->btc', q_lat, w_uq, preferred_element_type=jnp.float32)  59 us
    unnamed x19, local copies, waits for them, and re-layouts  50.5 us
  transfers between devices with their start and end apart: 5, of which 5 were waited for; matrix products, arithmetic and copies ran while one was open for 7% of the time, Pallas kernels for 0%

commit v1 on v0

v1 whole, which is shorter than its diff:
```python
import functools

import jax
import jax.numpy as jnp
import numpy as np
from jax import lax
from jax.experimental import pallas as pl
from jax.experimental.pallas import tpu as pltpu
from jax.sharding import PartitionSpec as P

EPSILON = 1e-6
ROPE_THETA = 10000.0
MESH = pl.DeviceIdType.MESH
F32 = jnp.float32
BF16 = jnp.bfloat16

RX, RY, RD, RP = 0, 1, 2, 3

N_DEV = 8
LOOKAHEAD = 3


def rope_consts(seq_len, rope_dim):
    half = rope_dim // 2
    inv_freq = (ROPE_THETA ** (-2.0 * np.arange(half, dtype=np.float32) / rope_dim)).astype(np.float32)
    angles = np.arange(seq_len, dtype=np.float32)[:, None] * inv_freq[None, :]
    cos_t = np.cos(angles).astype(np.float32)
    sin_t = np.sin(angles).astype(np.float32)
    cos2 = np.concatenate([cos_t, cos_t, cos_t, cos_t], axis=1)
    sin2 = np.concatenate([-sin_t, sin_t, -sin_t, sin_t], axis=1)
    return cos2, sin2


def rope128(v, cos2, sin2):
    lane = lax.broadcasted_iota(jnp.int32, v.shape, 1)
    swapped = jnp.where(lane % 64 < 32, pltpu.roll(v, 96, 1), pltpu.roll(v, 32, 1))
    return v * cos2 + swapped * sin2


def dot(a, b):
    return lax.dot_general(a, b, (((1,), (0,)), ((), ())), preferred_element_type=F32)


def dot_nt(a, b):
    return lax.dot_general(a, b, (((1,), (1,)), ((), ())), preferred_element_type=F32)


def block_kernel(
    cfg,
    x_hbm, gains_hbm, w_dq, w_uq, w_dkv, w_ukv, w_o, cos_hbm, sin_hbm,
    y_hbm, c_hbm, r_hbm, g_dq, g_uq, g_dkv, g_ukv, g_o,
    ao, qd, cq, c_s, r_lo, r_hi, r_out, cos_s, sin_s, gbuf, g1row, gqrow, gkvrow,
    wkv, wbig, wuq, wukv, q4, kv4, xres, yout,
    send_sem, recv_sem, load_sem, x_sem, y_sem, misc_sem, gain_send, gain_recv,
):
    tok = cfg["tok"]
    seq = cfg["seq"]
    width = cfg["width"]
    q_rank = cfg["q_rank"]
    kv_rank = cfg["kv_rank"]
    kdim = cfg["kdim"]
    n_dq, n_u, n_o = cfg["n_dq"], cfg["n_u"], cfg["n_o"]
    dq_w, o_w = cfg["dq_w"], cfg["o_w"]
    uq_w, ukv_w = cfg["uq_w"], cfg["ukv_w"]
    score_scale = cfg["score_scale"]
    first_u = 1 + n_dq
    first_o = first_u + n_u
    n_ticks = first_o + n_o

    me = lax.axis_index("fsdp")
    xn, yn, pt = me ^ 2, me ^ 4, me ^ 1

    def dev(t):
        return (lax.axis_index("dp"), t)

    barrier = pltpu.get_barrier_semaphore()
    for k in range(1, N_DEV):
        pl.semaphore_signal(barrier, inc=1, device_id=dev(me ^ k), device_id_type=MESH)
    pl.semaphore_wait(barrier, N_DEV - 1)

    gain_copies = []
    for k in range(1, N_DEV):
        gain_copies.append(pltpu.make_async_remote_copy(
            src_ref=gains_hbm.at[0], dst_ref=gbuf.at[me], send_sem=gain_send.at[k], recv_sem=gain_recv.at[k],
            device_id=dev(me ^ k), device_id_type=MESH))
        gain_copies[-1].start()

    class Piece:
        def __init__(self, local, full, n, cid, c0, w):
            self.local, self.full, self.n, self.cid = local, full, n, cid
            self.cols = pl.ds(pl.multiple_of(c0, 128), w)

        def shard(self, s, r0=0, nr=None):
            nr = self.n if nr is None else nr
            return self.full.at[pl.ds(pl.multiple_of(s * self.n + r0, 16), nr), self.cols]

        def remote(self, src, dst, k, t):
            return pltpu.make_async_remote_copy(
                src_ref=src, dst_ref=dst, send_sem=send_sem.at[self.cid], recv_sem=recv_sem.at[self.cid, k],
                device_id=dev(t), device_id_type=MESH)

        def send_own(self):
            for k, t in ((RX, xn), (RY, yn), (RP, pt)):
                self.remote(self.local.at[:, self.cols], self.shard(me), k, t).start()

        def on_xy(self):
            half = self.n // 2
            sx, sy = self.shard(xn), self.shard(yn)
            self.remote(sx, sx, RX, xn).wait_recv()
            s = self.shard(xn, 0, half)
            self.remote(s, s, RD, yn).start()
            self.remote(sx, sx, RP, pt).start()
            self.remote(sy, sy, RY, yn).wait_recv()
            s = self.shard(yn, half, half)
            self.remote(s, s, RD, xn).start()
            self.remote(sy, sy, RP, pt).start()

        def on_d(self):
            s = self.shard(me ^ 6)
            self.remote(s, s, RD, pt).wait_recv()
            self.remote(s, s, RP, pt).start()

        def on_p(self):
            s = self.full.at[pl.ds(0, 4 * self.n), self.cols]
            self.remote(s, s, RP, pt).wait_recv()

        def drain(self):
            s = self.full.at[pl.ds(0, 7 * self.n), self.cols]
            self.remote(s, s, RP, pt).wait_send()

        def load(self, buf, sem):
            for k in range(N_DEV):
                s = me ^ k
                src = self.local.at[:, self.cols] if k == 0 else self.shard(s)
                pltpu.make_async_copy(src, buf.at[pl.ds(pl.multiple_of(s * self.n, 16), self.n), :], sem).start()

        def wait_load(self, buf, sem):
            d = buf.at[pl.ds(0, N_DEV * self.n), :]
            pltpu.make_async_copy(d, d, sem).wait()

    def kv_pieces(_):
        return [Piece(w_dkv, g_dkv, w_dkv.shape[0], 0, 0, w_dkv.shape[1])]

    def dq_pieces(c):
        return [Piece(w_dq, g_dq, w_dq.shape[0], 1 + c, c * dq_w, dq_w)]

    def u_pieces(g):
        return [
            Piece(w_ukv, g_ukv, w_ukv.shape[0], first_u + 2 * g, g * ukv_w, ukv_w),
            Piece(w_uq, g_uq, w_uq.shape[0], first_u + 2 * g + 1, g * uq_w, uq_w),
        ]

    def o_pieces(n):
        return [Piece(w_o, g_o, w_o.shape[0], first_u + 2 * n_u + n, n * o_w, o_w)]

    def kv_bufs(_):
        return [(wkv, load_sem.at[4])]

    def dq_bufs(c):
        s = c % 2
        return [(wbig.at[s], load_sem.at[s])]

    def u_bufs(g):
        s = g % 2
        return [(wukv.at[s], load_sem.at[5 + s]), (wuq.at[s], load_sem.at[2 + s])]

    kinds = [
        (0, 1, kv_pieces, kv_bufs),
        (1, n_dq, dq_pieces, dq_bufs),
        (first_u, n_u, u_pieces, u_bufs),
        (first_o, n_o, o_pieces, dq_bufs),
    ]

    def each_kind(i, fn):
        for k, (first, count, _, _) in enumerate(kinds):
            @pl.when((i >= first) & (i < first + count))
            def _():
                fn(k, i - first)

    def send_own(k, c):
        for p in kinds[k][2](c):
            p.send_own()

    def on_xy(k, c):
        for p in kinds[k][2](c):
            p.on_xy()

    def arrive(k, c):
        for p in kinds[k][2](c):
            p.on_d()
        for p in kinds[k][2](c):
            p.on_p()
        if cfg["compute"]:
            for p, (buf, sem) in zip(kinds[k][2](c), kinds[k][3](c)):
                p.load(buf, sem)
            if k == 3:
                s = c % 2
                pltpu.make_async_copy(
                    x_hbm.at[:, pl.ds(pl.multiple_of(c * o_w, 128), o_w)], xres.at[s], x_sem.at[s]).start()

    mb = cfg["mb"]
    n_mb = tok // mb

    def compute_kv(_):
        def body(m, carry):
            rows = pl.ds(pl.multiple_of(m * mb, mb), mb)
            u = dot(ao[rows, 0:width], wkv[...])
            lat = u[:, 0:kv_rank]
            inv = lax.rsqrt(jnp.mean(lat * lat, axis=-1, keepdims=True) + EPSILON)
            c_s[rows, :] = (lat * inv * gkvrow[...]).astype(BF16)
            pe = jnp.concatenate([u[:, kv_rank:], jnp.zeros((mb, 64), F32)], axis=1)
            trows = pl.ds(pl.multiple_of((m * mb) % seq, mb), mb)
            rot = rope128(pe, cos_s[trows, :], sin_s[trows, :])
            r_lo[rows, :] = rot.astype(BF16)
            r_hi[rows, :] = pltpu.roll(rot, 64, 1).astype(BF16)
            r_out[rows, :] = rot[:, 0:64].astype(BF16)
            return carry

        lax.fori_loop(0, n_mb, body, 0)
        pltpu.make_async_copy(c_s, c_hbm, misc_sem.at[0]).start()
        pltpu.make_async_copy(r_out, r_hbm, misc_sem.at[1]).start()

    def compute_dq(c):
        slot = c % 2
        cols = pl.ds(pl.multiple_of(c * dq_w, 128), dq_w)

        def body(m, carry):
            rows = pl.ds(pl.multiple_of(m * mb, mb), mb)
            qd[rows, cols] = dot(ao[rows, 0:width], wbig[slot, 0:width, :])
            return carry

        lax.fori_loop(0, n_mb, body, 0)

        @pl.when(c == n_dq - 1)
        def _():
            def norm(m, carry):
                rows = pl.ds(pl.multiple_of(m * 32, 32), 32)
                v = qd[rows, :]
                inv = lax.rsqrt(jnp.mean(v * v, axis=-1, keepdims=True) + EPSILON)
                cq[rows, :] = (v * inv * gqrow[...]).astype(BF16)
                return carry

            lax.fori_loop(0, tok // 32, norm, 0)

    def compute_u(g):
        slot = g % 2

        def proj(m, carry):
            rows = pl.ds(pl.multiple_of(m * mb, mb), mb)
            trows = pl.ds(pl.multiple_of((m * mb) % seq, mb), mb)
            kv4[rows, :] = dot(c_s[rows, :], wukv[slot]).astype(BF16)
            q = dot(cq[rows, :], wuq[slot])
            cos2, sin2 = cos_s[trows, :], sin_s[trows, :]
            lane = lax.broadcasted_iota(jnp.int32, (mb, 128), 1)
            for p in range(uq_w // 384):
                b0 = q[:, 384 * p:384 * p + 128]
                b1 = q[:, 384 * p + 128:384 * p + 256]
                b2 = q[:, 384 * p + 256:384 * p + 384]
                q4[rows, 384 * p:384 * p + 128] = b0.astype(BF16)
                q4[rows, 384 * p + 128:384 * p + 256] = jnp.where(lane < 64, rope128(b1, cos2, sin2), b1).astype(BF16)
                q4[rows, 384 * p + 256:384 * p + 384] = jnp.where(lane < 64, b2, rope128(b2, cos2, sin2)).astype(BF16)
            return carry

        lax.fori_loop(0, n_mb, proj, 0)

        n_pairs = uq_w // 384
        qb_rows = 256

        def attn(t, carry):
            b, p = t // n_pairs, t % n_pairs
            brow = pl.multiple_of(b * seq, seq)
            rows = pl.ds(brow, seq)
            for hh in range(2):
                koff = pl.multiple_of(p * 512 + hh * 256, 128)
                k = kv4[rows, pl.ds(koff, 128)]
                v = kv4[rows, pl.ds(pl.multiple_of(koff + 128, 128), 128)]
                if hh == 0:
                    k_a, k_b = k, r_lo[rows, :]
                else:
                    lane = lax.broadcasted_iota(jnp.int32, (seq, 128), 1)
                    kr = pltpu.roll(k.astype(F32), 64, 1)
                    k_a = jnp.where(lane < 64, 0.0, kr).astype(BF16)
                    k_b = jnp.where(lane < 64, kr, r_hi[rows, :].astype(F32)).astype(BF16)
                kcat = jnp.concatenate([k_a, k_b], axis=1)
                for qb in range(seq // qb_rows):
                    nk = qb_rows * (qb + 1)
                    qrow = pl.ds(pl.multiple_of(brow + qb * qb_rows, qb_rows), qb_rows)
                    q = q4[qrow, pl.ds(pl.multiple_of(p * 384 + hh * 128, 128), 256)]
                    s = dot_nt(q, kcat[0:nk, :]) * (score_scale * 1.4426950408889634)
                    row = lax.broadcasted_iota(jnp.int32, (qb_rows, nk), 0) + qb * qb_rows
                    col = lax.broadcasted_iota(jnp.int32, (qb_rows, nk), 1)
                    s = jnp.where(row >= col, s, -1e30)
                    e = jnp.exp2(s - jnp.max(s, axis=-1, keepdims=True))
                    probs = (e * (1.0 / jnp.sum(e, axis=-1, keepdims=True))).astype(BF16)
                    o = dot(probs, v[0:nk, :])
                    ocol = pl.multiple_of((g * n_pairs * 2 + p * 2 + hh) * 128, 128)
                    ao[qrow, pl.ds(ocol, 128)] = o.astype(BF16)
            return carry

        lax.fori_loop(0, (tok // seq) * n_pairs, attn, 0)

    def y_copy(c, slot):
        return pltpu.make_async_copy(
            yout.at[slot], y_hbm.at[:, pl.ds(pl.multiple_of(c * o_w, 128), o_w)], y_sem.at[slot])

    def compute_o(c):
        slot = c % 2
        pltpu.make_async_copy(xres.at[slot], xres.at[slot], x_sem.at[slot]).wait()

        @pl.when(c >= 2)
        def _():
            y_copy(c - 2, slot).wait()

        def body(m, carry):
            rows = pl.ds(pl.multiple_of(m * mb, mb), mb)
            acc = dot(ao[rows, 0:kdim], wbig[slot])
            yout[slot, rows, :] = (xres[slot, rows, :].astype(F32) + acc).astype(BF16)
            return carry

        lax.fori_loop(0, n_mb, body, 0)
        y_copy(c, slot).start()

    def compute(k, c):
        for p, (buf, sem) in zip(kinds[k][2](c), kinds[k][3](c)):
            p.wait_load(buf, sem)
        (compute_kv, compute_dq, compute_u, compute_o)[k](c)

    for i in range(LOOKAHEAD):
        for k, (first, count, _, _) in enumerate(kinds):
            if first <= i < first + count:
                send_own(k, i - first)

    local = [
        pltpu.make_async_copy(gains_hbm.at[0], gbuf.at[me], misc_sem.at[2]),
        pltpu.make_async_copy(cos_hbm, cos_s, misc_sem.at[3]),
        pltpu.make_async_copy(sin_hbm, sin_s, misc_sem.at[4]),
        pltpu.make_async_copy(x_hbm, ao.at[:, pl.ds(0, width)], misc_sem.at[5]),
    ]
    for cp in local:
        cp.start()
    for cp in local:
        cp.wait()
    for k in range(1, N_DEV):
        gain_copies[k - 1].wait()

    n1, nq, nkv = width // N_DEV, q_rank // N_DEV, kv_rank // N_DEV
    for j in range(N_DEV):
        g1row[:, n1 * j:n1 * (j + 1)] = gbuf[j, :, 0:n1]
    gqrow[...] = jnp.concatenate([gbuf[j, :, n1:n1 + nq] for j in range(N_DEV)], axis=1)
    gkvrow[...] = jnp.concatenate([gbuf[j, :, n1 + nq:n1 + nq + nkv] for j in range(N_DEV)], axis=1)

    if cfg["compute"]:
        def norm_x(m, carry):
            rows = pl.ds(pl.multiple_of(m * 16, 16), 16)
            v = ao[rows, 0:width].astype(F32)
            inv = lax.rsqrt(jnp.mean(v * v, axis=-1, keepdims=True) + EPSILON)
            ao[rows, 0:width] = (v * inv * g1row[...]).astype(BF16)
            return carry

        lax.fori_loop(0, tok // 16, norm_x, 0)

    def tick(i, carry):
        each_kind(i, on_xy)
        each_kind(i + LOOKAHEAD, send_own)
        each_kind(i - 1, arrive)
        if cfg["compute"]:
            each_kind(i - 2, compute)
        return carry

    lax.fori_loop(0, n_ticks + 2, tick, 0)

    def drain(i, carry):
        each_kind(i, lambda k, c: [p.drain() for p in kinds[k][2](c)])
        return carry

    lax.fori_loop(0, n_ticks, drain, 0)
    if cfg["compute"]:
        pltpu.make_async_copy(c_s, c_hbm, misc_sem.at[0]).wait()
        pltpu.make_async_copy(r_out, r_hbm, misc_sem.at[1]).wait()
        y_copy(n_o - 2, (n_o - 2) % 2).wait()
        y_copy(n_o - 1, (n_o - 1) % 2).wait()


def solution(mesh, compute=True):
    batch_spec = P(("dp", "fsdp"))
    row_spec = P("fsdp")
    mat_spec = P("fsdp", None)

    def run_block(tokens, gain_in, w_dq, gain_q, w_uq, w_dkv, gain_kv, w_ukv, w_out):
        seq = tokens.shape[1]
        rope_dim = w_dkv.shape[1] - gain_kv.shape[0]
        nope_total = w_ukv.shape[1] - w_out.shape[0]
        n_heads = (w_uq.shape[1] - nope_total) // rope_dim
        cos2, sin2 = rope_consts(seq, rope_dim)

        def local_block(tok_blk, g1, wdq, gq, wuq, wdkv, gkv, wukv, wo):
            n_prompts, _, width = tok_blk.shape
            tok = n_prompts * seq
            q_rank, kv_rank = gain_q.shape[0], gain_kv.shape[0]
            heads_per = 4
            cfg = dict(
                tok=tok, seq=seq, width=width, q_rank=q_rank, kv_rank=kv_rank, kdim=w_out.shape[0],
                n_dq=q_rank // 256, n_u=n_heads // heads_per, n_o=width // 256, dq_w=256, o_w=256,
                uq_w=heads_per * (w_uq.shape[1] // n_heads), ukv_w=heads_per * (w_ukv.shape[1] // n_heads),
                score_scale=(w_uq.shape[1] // n_heads) ** -0.5, mb=256, compute=compute,
            )
            n_sems = 1 + cfg["n_dq"] + 2 * cfg["n_u"] + cfg["n_o"]
            gains = jnp.concatenate([g1, gq, gkv]).astype(F32).reshape(1, 1, -1)
            n_g = gains.shape[2]
            any_spec = pl.BlockSpec(memory_space=pl.ANY)
            outs = pl.pallas_call(
                functools.partial(block_kernel, cfg),
                out_shape=[
                    jax.ShapeDtypeStruct((tok, width), BF16),
                    jax.ShapeDtypeStruct((tok, kv_rank), BF16),
                    jax.ShapeDtypeStruct((tok, rope_dim), BF16),
                    jax.ShapeDtypeStruct(w_dq.shape, BF16),
                    jax.ShapeDtypeStruct(w_uq.shape, BF16),
                    jax.ShapeDtypeStruct(w_dkv.shape, BF16),
                    jax.ShapeDtypeStruct(w_ukv.shape, BF16),
                    jax.ShapeDtypeStruct(w_out.shape, BF16),
                ],
                in_specs=[any_spec] * 9,
                out_specs=[any_spec] * 8,
                scratch_shapes=[
                    pltpu.VMEM((tok, cfg["kdim"]), BF16),
                    pltpu.VMEM((tok, q_rank), F32),
                    pltpu.VMEM((tok, q_rank), BF16),
                    pltpu.VMEM((tok, kv_rank), BF16),
                    pltpu.VMEM((tok, 128), BF16),
                    pltpu.VMEM((tok, 128), BF16),
                    pltpu.VMEM((tok, rope_dim), BF16),
                    pltpu.VMEM((seq, 128), F32),
                    pltpu.VMEM((seq, 128), F32),
                    pltpu.VMEM((N_DEV, 1, n_g), F32),
                    pltpu.VMEM((1, width), F32),
                    pltpu.VMEM((1, q_rank), F32),
                    pltpu.VMEM((1, kv_rank), F32),
                    pltpu.VMEM(w_dkv.shape, BF16),
                    pltpu.VMEM((2, cfg["kdim"], 256), BF16),
                    pltpu.VMEM((2, q_rank, cfg["uq_w"]), BF16),
                    pltpu.VMEM((2, kv_rank, cfg["ukv_w"]), BF16),
                    pltpu.VMEM((tok, cfg["uq_w"]), BF16),
                    pltpu.VMEM((tok, cfg["ukv_w"]), BF16),
                    pltpu.VMEM((2, tok, 256), BF16),
                    pltpu.VMEM((2, tok, 256), BF16),
                    pltpu.SemaphoreType.DMA((n_sems,)),
                    pltpu.SemaphoreType.DMA((n_sems, 4)),
                    pltpu.SemaphoreType.DMA((7,)),
                    pltpu.SemaphoreType.DMA((2,)),
                    pltpu.SemaphoreType.DMA((2,)),
                    pltpu.SemaphoreType.DMA((6,)),
                    pltpu.SemaphoreType.DMA((N_DEV,)),
                    pltpu.SemaphoreType.DMA((N_DEV,)),
                ],
                compiler_params=pltpu.CompilerParams(
                    collective_id=0, has_side_effects=True, vmem_limit_bytes=66_000_000),
                name="mla_block",
            )(tok_blk.reshape(tok, width), gains, wdq, wuq, wdkv, wukv, wo, jnp.asarray(cos2), jnp.asarray(sin2))
            y, c, r = outs[:3]
            return (y.reshape(tok_blk.shape), c.reshape(n_prompts, seq, kv_rank), r.reshape(n_prompts, seq, rope_dim))

        return jax.shard_map(
            local_block,
            mesh=mesh,
            in_specs=(batch_spec, row_spec, mat_spec, row_spec, mat_spec, mat_spec, row_spec, mat_spec, mat_spec),
            out_specs=(batch_spec, batch_spec, batch_spec),
            check_vma=False,
        )(tokens, gain_in, w_dq, gain_q, w_uq, w_dkv, gain_kv, w_ukv, w_out)

    return run_block
```

time: 1560 us -> 880 us (0.56)
  Pallas kernels: 0 us -> 858 us
  waiting for transfers between devices: 794 us -> 0 us
  matrix products: 490 us -> 0 us
  local copies, waits for them, and re-layouts: 112 us -> 20.5 us
  other arithmetic: 84.9 us -> 0.6 us
  blocking collectives: 38.1 us -> 0 us
  loops' own time: 19.4 us -> 0 us
    pallas_call x0 -> x1, Pallas kernels: none -> 858 us  [local_block(): pl.pallas_call(functools.partial(block_kernel, cfg), out_shape=[jax.Shape...]
    all_gather x5 -> x0, waiting for transfers between devices: 790 us -> none  [the longest x1 512 us: local_block(): w_out_all = lax.all_gather(w_out_s, 'fsdp', tiled=True)]
    dot_general x14 -> x0, matrix products: 490 us -> none  [the longest x2 143 us: attend(): jnp.einsum('btc,cd->btd', attn_out, w_out, preferred_element_type=jnp.flo...]
    reduce_sum x4 -> x0, other arithmetic: 50.4 us -> none  [the longest x2 42.1 us: attend(): attn_probs = jax.nn.softmax(scores, axis=-1).astype(jnp.bfloat16)]
    while x20 -> x0, local copies, waits for them, and re-layouts: 46.3 us -> none
    unnamed x19 -> x6, local copies, waits for them, and re-layouts: 50.5 us -> 18.4 us
    unnamed x1 -> x0, blocking collectives: 25.6 us -> none
    convert_element_type x6 -> x1, other arithmetic: 23.5 us -> 0.6 us  [local_block(): gains = jnp.concatenate([g1, gq, gkv]).astype(F32).reshape(1, 1, -1)]
  transfers between devices with their start and end apart: 5 -> 0, of which waited for: 5 -> 0; matrix products, arithmetic and copies ran while one was open for 7% -> 0% of each run, Pallas kernels for 0% -> 0%
where the time goes in v1:
time: 880 us; the launch traced here: 879 us
  Pallas kernels  858 us (98%)
  local copies, waits for them, and re-layouts  20.5 us (2%)
    pallas_call x1, Pallas kernels, local_block(): pl.pallas_call(functools.partial(block_kernel, cfg), out_shape=[jax.Shape...  858 us
    unnamed x6, local copies, waits for them, and re-layouts  18.4 us

profile of v1, /device:TPU:0, one launch (start us, length us, event | category | flops | bytes accessed | tf_op | source)
XLA Modules:
  0.0 879.2 jit_solution(3947660424651287625)
XLA Ops:
  0.6 0.7 concatenate.17
  1.3 0.7 concatenate.16
  2.0 0.7 concatenate.19
  2.7 0.6 convert_element_type.10.gains_hbm
  3.3 2.3 copy.14.w_dkv
  5.7 857.6 %mla_block.1 = (bf16[1024,7168]{1,0:T(8,128)(2,1)}, bf16[1024,512]{1,0:T(8,128)(2,1)}, bf16[1024,64]{1,0:T(8,128)(2,1)}, bf16[7168,1536]{1,0:T(8,128)(2,1)}, bf1...) custom-call(bf16[1024,7168]{1,0:T(8,128)(2,1)} %bitcast.6, ...), custom_call_target="tpu_custom_call" | custom-call | tf_op jit(solution)/shard_map/mla_block/pallas_call | solution.py:411
  863.2 1.7 copy.15
  865.0 0.0 copy-start
  865.0 13.3 %copy.18 = bf16[2,512,7168]{2,1,0:T(8,128)(2,1)} copy(bf16[2,512,7168]{2,1,0:T(8,128)(2,1)} %bitcast.5) | data formatting | bytes 29360128
  878.3 0.0 copy-done
  878.3 1.0 copy.19
Async XLA Ops:
  865.0 13.3 %copy-start = (bf16[1024,512]{1,0:T(8,128)(2,1)S(1)}, bf16[1024,512]{1,0:T(8,128)(2,1)}, u32[]{:S(2)}) copy-start(bf16[1024,512]{1,0:T(8,128)(2,1)} %get-tuple-element.7) | copy-start | bytes 3145732

commit v2 on v1

--- a/solution.py
+++ b/solution.py
@@ -14,10 +14,11 @@
 F32 = jnp.float32
 BF16 = jnp.bfloat16
 
-RX, RY, RD, RP = 0, 1, 2, 3
+RX, RY, RD, RP, RPD = 0, 1, 2, 3, 4
 
 N_DEV = 8
 LOOKAHEAD = 3
+LAG = 4
 
 
 def rope_consts(seq_len, rope_dim):
@@ -50,7 +51,7 @@
     x_hbm, gains_hbm, w_dq, w_uq, w_dkv, w_ukv, w_o, cos_hbm, sin_hbm,
     y_hbm, c_hbm, r_hbm, g_dq, g_uq, g_dkv, g_ukv, g_o,
     ao, qd, cq, c_s, r_lo, r_hi, r_out, cos_s, sin_s, gbuf, g1row, gqrow, gkvrow,
-    wkv, wbig, wuq, wukv, q4, kv4, xres, yout,
+    wkv, wbig, wuq, wukv, q4, kv4, acc, xres, yout,
     send_sem, recv_sem, load_sem, x_sem, y_sem, misc_sem, gain_send, gain_recv,
 ):
     tok = cfg["tok"]
@@ -87,12 +88,21 @@
 
     class Piece:
         def __init__(self, local, full, n, cid, c0, w):
-            self.local, self.full, self.n, self.cid = local, full, n, cid
+            self.local_ref, self.full, self.n, self.cid = local, full, n, cid
             self.cols = pl.ds(pl.multiple_of(c0, 128), w)
 
-        def shard(self, s, r0=0, nr=None):
-            nr = self.n if nr is None else nr
+        def local(self):
+            return self.local_ref.at[:, self.cols]
+
+        def shard(self, s, half=None):
+            r0, nr = (0, self.n) if half is None else (half * (self.n // 2), self.n // 2)
             return self.full.at[pl.ds(pl.multiple_of(s * self.n + r0, 16), nr), self.cols]
+
+        def shards(self, count):
+            return self.full.at[pl.ds(0, count * self.n), self.cols]
+
+        def dst(self, buf, slot):
+            return buf.at[pl.ds(pl.multiple_of(slot * self.n, 16), self.n), :]
 
         def remote(self, src, dst, k, t):
             return pltpu.make_async_remote_copy(
@@ -101,45 +111,58 @@
 
         def send_own(self):
             for k, t in ((RX, xn), (RY, yn), (RP, pt)):
-                self.remote(self.local.at[:, self.cols], self.shard(me), k, t).start()
+                self.remote(self.local(), self.shard(me), k, t).start()
 
         def on_xy(self):
-            half = self.n // 2
-            sx, sy = self.shard(xn), self.shard(yn)
-            self.remote(sx, sx, RX, xn).wait_recv()
-            s = self.shard(xn, 0, half)
-            self.remote(s, s, RD, yn).start()
-            self.remote(sx, sx, RP, pt).start()
-            self.remote(sy, sy, RY, yn).wait_recv()
-            s = self.shard(yn, half, half)
-            self.remote(s, s, RD, xn).start()
-            self.remote(sy, sy, RP, pt).start()
+            for h, k, src, other in ((0, RX, xn, yn), (1, RY, yn, xn)):
+                s = self.shard(src)
+                self.remote(s, s, k, src).wait_recv()
+                f = self.shard(src, h)
+                self.remote(f, f, RD, other).start()
+                self.remote(s, s, RP, pt).start()
 
         def on_d(self):
             s = self.shard(me ^ 6)
             self.remote(s, s, RD, pt).wait_recv()
-            self.remote(s, s, RP, pt).start()
-
-        def on_p(self):
-            s = self.full.at[pl.ds(0, 4 * self.n), self.cols]
+            self.remote(s, s, RPD, pt).start()
+
+        def wait_p(self):
+            s = self.shards(3)
             self.remote(s, s, RP, pt).wait_recv()
 
+        def wait_pd(self):
+            s = self.shards(1)
+            self.remote(s, s, RPD, pt).wait_recv()
+
         def drain(self):
-            s = self.full.at[pl.ds(0, 7 * self.n), self.cols]
+            s = self.shards(7)
             self.remote(s, s, RP, pt).wait_send()
 
-        def load(self, buf, sem):
-            for k in range(N_DEV):
-                s = me ^ k
-                src = self.local.at[:, self.cols] if k == 0 else self.shard(s)
-                pltpu.make_async_copy(src, buf.at[pl.ds(pl.multiple_of(s * self.n, 16), self.n), :], sem).start()
-
-        def wait_load(self, buf, sem):
-            d = buf.at[pl.ds(0, N_DEV * self.n), :]
-            pltpu.make_async_copy(d, d, sem).wait()
+        def load(self, buf, sem, ks, relative=False):
+            for k in ks:
+                src = self.local() if k == 0 else self.shard(me ^ k)
+                pltpu.make_async_copy(src, self.dst(buf, k if relative else me ^ k), sem).start()
+
+    class ColumnPiece(Piece):
+        def local(self):
+            return self.local_ref
+
+        def shard(self, s, half=None):
+            rows = self.full.shape[0]
+            r0, nr = (0, rows) if half is None else (half * (rows // 2), rows // 2)
+            return self.full.at[pl.ds(r0, nr), pl.ds(pl.multiple_of(s * self.n, 128), self.n)]
+
+        def shards(self, count):
+            return self.full.at[:, pl.ds(0, count * self.n)]
+
+        def dst(self, buf, slot):
+            return buf.at[:, pl.ds(pl.multiple_of(slot * self.n, 128), self.n)]
+
+    def wait_loaded(ref, sem):
+        pltpu.make_async_copy(ref, ref, sem).wait()
 
     def kv_pieces(_):
-        return [Piece(w_dkv, g_dkv, w_dkv.shape[0], 0, 0, w_dkv.shape[1])]
+        return [ColumnPiece(w_dkv, g_dkv, w_dkv.shape[1], 0, 0, 128)]
 
     def dq_pieces(c):
         return [Piece(w_dq, g_dq, w_dq.shape[0], 1 + c, c * dq_w, dq_w)]
@@ -162,17 +185,17 @@
 
     def u_bufs(g):
         s = g % 2
-        return [(wukv.at[s], load_sem.at[5 + s]), (wuq.at[s], load_sem.at[2 + s])]
+        return [(wukv.at[s], load_sem.at[5 + s]), (wuq.at[s], load_sem.at[7 + s])]
 
     kinds = [
         (0, 1, kv_pieces, kv_bufs),
         (1, n_dq, dq_pieces, dq_bufs),
         (first_u, n_u, u_pieces, u_bufs),
-        (first_o, n_o, o_pieces, dq_bufs),
+        (first_o, n_o, o_pieces, None),
     ]
 
-    def each_kind(i, fn):
-        for k, (first, count, _, _) in enumerate(kinds):
+    def each_kind(i, fn, which=None):
+        for k, (first, count, _, _) in enumerate(kinds if which is None else which):
             @pl.when((i >= first) & (i < first + count))
             def _():
                 fn(k, i - first)
@@ -185,26 +208,30 @@
         for p in kinds[k][2](c):
             p.on_xy()
 
-    def arrive(k, c):
+    def on_d(k, c):
         for p in kinds[k][2](c):
             p.on_d()
-        for p in kinds[k][2](c):
-            p.on_p()
+
+    def arrive(k, c):
+        ps = kinds[k][2](c)
+        if cfg["comm"]:
+            for p in ps:
+                p.wait_p()
+                p.wait_pd()
         if cfg["compute"]:
-            for p, (buf, sem) in zip(kinds[k][2](c), kinds[k][3](c)):
-                p.load(buf, sem)
-            if k == 3:
-                s = c % 2
-                pltpu.make_async_copy(
-                    x_hbm.at[:, pl.ds(pl.multiple_of(c * o_w, 128), o_w)], xres.at[s], x_sem.at[s]).start()
+            for p, (buf, sem) in zip(ps, kinds[k][3](c)):
+                p.load(buf, sem, range(N_DEV))
 
     mb = cfg["mb"]
     n_mb = tok // mb
+    rows_o = kdim // N_DEV
+    heads_dev = rows_o // 128
+    near = 6 * rows_o
 
     def compute_kv(_):
         def body(m, carry):
             rows = pl.ds(pl.multiple_of(m * mb, mb), mb)
-            u = dot(ao[rows, 0:width], wkv[...])
+            u = dot_nt(ao[rows, 0:width], wkv[...])
             lat = u[:, 0:kv_rank]
             inv = lax.rsqrt(jnp.mean(lat * lat, axis=-1, keepdims=True) + EPSILON)
             c_s[rows, :] = (lat * inv * gkvrow[...]).astype(BF16)
@@ -213,7 +240,7 @@
             rot = rope128(pe, cos_s[trows, :], sin_s[trows, :])
             r_lo[rows, :] = rot.astype(BF16)
             r_hi[rows, :] = pltpu.roll(rot, 64, 1).astype(BF16)
-            r_out[rows, :] = rot[:, 0:64].astype(BF16)
+            r_out[(m * mb) // seq, :, trows] = rot.T[0:64, :].astype(BF16)
             return carry
 
         lax.fori_loop(0, n_mb, body, 0)
@@ -286,14 +313,21 @@
                     nk = qb_rows * (qb + 1)
                     qrow = pl.ds(pl.multiple_of(brow + qb * qb_rows, qb_rows), qb_rows)
                     q = q4[qrow, pl.ds(pl.multiple_of(p * 384 + hh * 128, 128), 256)]
-                    s = dot_nt(q, kcat[0:nk, :]) * (score_scale * 1.4426950408889634)
-                    row = lax.broadcasted_iota(jnp.int32, (qb_rows, nk), 0) + qb * qb_rows
-                    col = lax.broadcasted_iota(jnp.int32, (qb_rows, nk), 1)
-                    s = jnp.where(row >= col, s, -1e30)
-                    e = jnp.exp2(s - jnp.max(s, axis=-1, keepdims=True))
-                    probs = (e * (1.0 / jnp.sum(e, axis=-1, keepdims=True))).astype(BF16)
+                    scale = score_scale * 1.4426950408889634
+                    row = lax.broadcasted_iota(jnp.int32, (qb_rows, qb_rows), 0)
+                    col = lax.broadcasted_iota(jnp.int32, (qb_rows, qb_rows), 1)
+                    s = dot_nt(q, kcat[0:nk, :]) * scale
+                    parts = [jnp.where(row >= col, s[:, nk - qb_rows:], -1e30)]
+                    if qb > 0:
+                        parts.insert(0, s[:, :nk - qb_rows])
+                    top = functools.reduce(jnp.maximum, [jnp.max(x, axis=-1, keepdims=True) for x in parts])
+                    exps = [jnp.exp2(x - top) for x in parts]
+                    inv = 1.0 / sum(jnp.sum(x, axis=-1, keepdims=True) for x in exps)
+                    probs = [(x * inv).astype(BF16) for x in exps]
+                    probs = probs[0] if qb == 0 else jnp.concatenate(probs, axis=1)
                     o = dot(probs, v[0:nk, :])
-                    ocol = pl.multiple_of((g * n_pairs * 2 + p * 2 + hh) * 128, 128)
+                    head = g * n_pairs * 2 + p * 2 + hh
+                    ocol = pl.multiple_of(((head // heads_dev) ^ me) * rows_o + (head % heads_dev) * 128, 128)
                     ao[qrow, pl.ds(ocol, 128)] = o.astype(BF16)
             return carry
 
@@ -303,29 +337,60 @@
         return pltpu.make_async_copy(
             yout.at[slot], y_hbm.at[:, pl.ds(pl.multiple_of(c * o_w, 128), o_w)], y_sem.at[slot])
 
-    def compute_o(c):
+    def o_near(c, carry):
         slot = c % 2
-        pltpu.make_async_copy(xres.at[slot], xres.at[slot], x_sem.at[slot]).wait()
+        buf = wbig.at[slot]
+        p = o_pieces(c)[0]
+        p.load(buf, load_sem.at[slot], (0, 2, 4), relative=True)
+        cols = pl.ds(pl.multiple_of(c * o_w, 128), o_w)
+        pltpu.make_async_copy(x_hbm.at[:, cols], xres.at[slot], x_sem.at[slot]).start()
+        if cfg["comm"]:
+            p.wait_p()
+        p.load(buf, load_sem.at[slot], (1, 3, 5), relative=True)
+        wait_loaded(buf.at[pl.ds(0, near), :], load_sem.at[slot])
+        wait_loaded(xres.at[slot], x_sem.at[slot])
+
+        def body(m, carry):
+            rows = pl.ds(pl.multiple_of(m * mb, mb), mb)
+            acc[c % 3, rows, :] = xres[slot, rows, :].astype(F32) + dot(ao[rows, 0:near], wbig[slot, 0:near, :])
+            return carry
+
+        lax.fori_loop(0, n_mb, body, 0)
+        return carry
+
+    def o_far(c, carry):
+        slot = c % 2
+        buf = wbig.at[slot]
+        p = o_pieces(c)[0]
+        p.load(buf, load_sem.at[2 + slot], (6,), relative=True)
+        if cfg["comm"]:
+            p.wait_pd()
+        p.load(buf, load_sem.at[2 + slot], (7,), relative=True)
 
         @pl.when(c >= 2)
         def _():
             y_copy(c - 2, slot).wait()
 
+        wait_loaded(buf.at[pl.ds(near, kdim - near), :], load_sem.at[2 + slot])
+
         def body(m, carry):
             rows = pl.ds(pl.multiple_of(m * mb, mb), mb)
-            acc = dot(ao[rows, 0:kdim], wbig[slot])
-            yout[slot, rows, :] = (xres[slot, rows, :].astype(F32) + acc).astype(BF16)
+            yout[slot, rows, :] = (
+                acc[c % 3, rows, :] + dot(ao[rows, near:kdim], wbig[slot, near:kdim, :])).astype(BF16)
             return carry
 
         lax.fori_loop(0, n_mb, body, 0)
         y_copy(c, slot).start()
+        return carry
 
     def compute(k, c):
-        for p, (buf, sem) in zip(kinds[k][2](c), kinds[k][3](c)):
-            p.wait_load(buf, sem)
-        (compute_kv, compute_dq, compute_u, compute_o)[k](c)
-
-    for i in range(LOOKAHEAD):
+        for (buf, sem) in kinds[k][3](c):
+            wait_loaded(buf.at[pl.ds(0, width), :] if k == 1 else buf, sem)
+        if k not in cfg["skip"]:
+            (compute_kv, compute_dq, compute_u)[k](c)
+
+    LA = cfg["lookahead"]
+    for i in range(LA if cfg["comm"] else 0):
         for k, (first, count, _, _) in enumerate(kinds):
             if first <= i < first + count:
                 send_own(k, i - first)
@@ -359,12 +424,27 @@
 
         lax.fori_loop(0, tok // 16, norm_x, 0)
 
+    def each_early(i, fn):
+        each_kind(i, fn, kinds[:3])
+
+    def near_done(n):
+        return jnp.clip(jnp.minimum(n + 1, 2 * (n - LAG + 1)), 0, n_o)
+
+    def far_done(n):
+        return jnp.clip(jnp.minimum(n - 1, near_done(n)), 0, n_o)
+
     def tick(i, carry):
-        each_kind(i, on_xy)
-        each_kind(i + LOOKAHEAD, send_own)
-        each_kind(i - 1, arrive)
+        if cfg["comm"]:
+            each_kind(i, on_xy)
+            each_kind(i + LA, send_own)
+            each_kind(i - 2, on_d)
+        each_early(i - 3, arrive)
         if cfg["compute"]:
-            each_kind(i - 2, compute)
+            each_early(i - LAG, compute)
+            if 3 not in cfg["skip"]:
+                n = i - first_o
+                lax.fori_loop(near_done(n - 1), near_done(n), o_near, 0)
+                lax.fori_loop(far_done(n - 1), far_done(n), o_far, 0)
         return carry
 
     lax.fori_loop(0, n_ticks + 2, tick, 0)
@@ -373,15 +453,44 @@
         each_kind(i, lambda k, c: [p.drain() for p in kinds[k][2](c)])
         return carry
 
-    lax.fori_loop(0, n_ticks, drain, 0)
+    if cfg["comm"]:
+        lax.fori_loop(0, n_ticks, drain, 0)
     if cfg["compute"]:
-        pltpu.make_async_copy(c_s, c_hbm, misc_sem.at[0]).wait()
-        pltpu.make_async_copy(r_out, r_hbm, misc_sem.at[1]).wait()
-        y_copy(n_o - 2, (n_o - 2) % 2).wait()
-        y_copy(n_o - 1, (n_o - 1) % 2).wait()
-
-
-def solution(mesh, compute=True):
+        if 0 not in cfg["skip"]: pltpu.make_async_copy(c_s, c_hbm, misc_sem.at[0]).wait()
+        if 0 not in cfg["skip"]: pltpu.make_async_copy(r_out, r_hbm, misc_sem.at[1]).wait()
+        if 3 not in cfg["skip"]: y_copy(n_o - 2, (n_o - 2) % 2).wait()
+        if 3 not in cfg["skip"]: y_copy(n_o - 1, (n_o - 1) % 2).wait()
+
+
+def copy_out_kernel(steps, y_in, c_in, r_in, y_out, c_out, r_out, y_buf, c_buf, r_buf, sem_in, sem_out):
+    n = y_in.shape[0] // steps
+    chunks = [(y_in.at[pl.ds(i * n, n)], y_buf.at[pl.ds(i * n, n)], y_out.at[pl.ds(i * n, n)]) for i in range(steps)]
+    chunks += [(c_in, c_buf, c_out), (r_in, r_buf, r_out)]
+    for i, (src, buf, _) in enumerate(chunks):
+        pltpu.make_async_copy(src, buf, sem_in.at[i]).start()
+    for i, (src, buf, dst) in enumerate(chunks):
+        pltpu.make_async_copy(src, buf, sem_in.at[i]).wait()
+        pltpu.make_async_copy(buf, dst, sem_out.at[i]).start()
+    for i, (_, buf, dst) in enumerate(chunks):
+        pltpu.make_async_copy(buf, dst, sem_out.at[i]).wait()
+
+
+def copy_out(y, c, r):
+    steps = 16
+    any_spec = pl.BlockSpec(memory_space=pl.ANY)
+    return pl.pallas_call(
+        functools.partial(copy_out_kernel, steps),
+        out_shape=[jax.ShapeDtypeStruct(v.shape, v.dtype) for v in (y, c, r)],
+        in_specs=[any_spec] * 3,
+        out_specs=[any_spec] * 3,
+        scratch_shapes=[pltpu.VMEM(v.shape, v.dtype) for v in (y, c, r)]
+        + [pltpu.SemaphoreType.DMA((steps + 2,)), pltpu.SemaphoreType.DMA((steps + 2,))],
+        compiler_params=pltpu.CompilerParams(vmem_limit_bytes=60_000_000),
+        name="copy_out",
+    )(y, c, r)
+
+
+def solution(mesh, compute=True, comm=True, lookahead=LOOKAHEAD, skip=()):
     batch_spec = P(("dp", "fsdp"))
     row_spec = P("fsdp")
     mat_spec = P("fsdp", None)
@@ -402,21 +511,21 @@
                 tok=tok, seq=seq, width=width, q_rank=q_rank, kv_rank=kv_rank, kdim=w_out.shape[0],
                 n_dq=q_rank // 256, n_u=n_heads // heads_per, n_o=width // 256, dq_w=256, o_w=256,
                 uq_w=heads_per * (w_uq.shape[1] // n_heads), ukv_w=heads_per * (w_ukv.shape[1] // n_heads),
-                score_scale=(w_uq.shape[1] // n_heads) ** -0.5, mb=256, compute=compute,
+                score_scale=(w_uq.shape[1] // n_heads) ** -0.5, mb=256, compute=compute, comm=comm, lookahead=lookahead, skip=skip,
             )
             n_sems = 1 + cfg["n_dq"] + 2 * cfg["n_u"] + cfg["n_o"]
-            gains = jnp.concatenate([g1, gq, gkv]).astype(F32).reshape(1, 1, -1)
-            n_g = gains.shape[2]
+            n_g = g1.shape[0] + gq.shape[0] + gkv.shape[0]
+            gains = jnp.concatenate([g1, gq, gkv]).astype(F32).reshape(1, 1, n_g)
             any_spec = pl.BlockSpec(memory_space=pl.ANY)
             outs = pl.pallas_call(
                 functools.partial(block_kernel, cfg),
                 out_shape=[
                     jax.ShapeDtypeStruct((tok, width), BF16),
                     jax.ShapeDtypeStruct((tok, kv_rank), BF16),
-                    jax.ShapeDtypeStruct((tok, rope_dim), BF16),
+                    jax.ShapeDtypeStruct((n_prompts, rope_dim, seq), BF16),
                     jax.ShapeDtypeStruct(w_dq.shape, BF16),
                     jax.ShapeDtypeStruct(w_uq.shape, BF16),
-                    jax.ShapeDtypeStruct(w_dkv.shape, BF16),
+                    jax.ShapeDtypeStruct(w_dkv.shape[::-1], BF16),
                     jax.ShapeDtypeStruct(w_ukv.shape, BF16),
                     jax.ShapeDtypeStruct(w_out.shape, BF16),
                 ],
@@ -429,24 +538,25 @@
                     pltpu.VMEM((tok, kv_rank), BF16),
                     pltpu.VMEM((tok, 128), BF16),
                     pltpu.VMEM((tok, 128), BF16),
-                    pltpu.VMEM((tok, rope_dim), BF16),
+                    pltpu.VMEM((n_prompts, rope_dim, seq), BF16),
                     pltpu.VMEM((seq, 128), F32),
                     pltpu.VMEM((seq, 128), F32),
                     pltpu.VMEM((N_DEV, 1, n_g), F32),
                     pltpu.VMEM((1, width), F32),
                     pltpu.VMEM((1, q_rank), F32),
                     pltpu.VMEM((1, kv_rank), F32),
-                    pltpu.VMEM(w_dkv.shape, BF16),
+                    pltpu.VMEM(w_dkv.shape[::-1], BF16),
                     pltpu.VMEM((2, cfg["kdim"], 256), BF16),
                     pltpu.VMEM((2, q_rank, cfg["uq_w"]), BF16),
                     pltpu.VMEM((2, kv_rank, cfg["ukv_w"]), BF16),
                     pltpu.VMEM((tok, cfg["uq_w"]), BF16),
                     pltpu.VMEM((tok, cfg["ukv_w"]), BF16),
+                    pltpu.VMEM((3, tok, 256), F32),
                     pltpu.VMEM((2, tok, 256), BF16),
                     pltpu.VMEM((2, tok, 256), BF16),
                     pltpu.SemaphoreType.DMA((n_sems,)),
-                    pltpu.SemaphoreType.DMA((n_sems, 4)),
-                    pltpu.SemaphoreType.DMA((7,)),
+                    pltpu.SemaphoreType.DMA((n_sems, 5)),
+                    pltpu.SemaphoreType.DMA((9,)),
                     pltpu.SemaphoreType.DMA((2,)),
                     pltpu.SemaphoreType.DMA((2,)),
                     pltpu.SemaphoreType.DMA((6,)),
@@ -456,9 +566,9 @@
                 compiler_params=pltpu.CompilerParams(
                     collective_id=0, has_side_effects=True, vmem_limit_bytes=66_000_000),
                 name="mla_block",
-            )(tok_blk.reshape(tok, width), gains, wdq, wuq, wdkv, wukv, wo, jnp.asarray(cos2), jnp.asarray(sin2))
-            y, c, r = outs[:3]
-            return (y.reshape(tok_blk.shape), c.reshape(n_prompts, seq, kv_rank), r.reshape(n_prompts, seq, rope_dim))
+            )(tok_blk.reshape(tok, width), gains, wdq, wuq, wdkv.T, wukv, wo, jnp.asarray(cos2), jnp.asarray(sin2))
+            y, c, r = copy_out(*outs[:3])
+            return (y.reshape(tok_blk.shape), c.reshape(n_prompts, seq, kv_rank), jnp.swapaxes(r, 1, 2))
 
         return jax.shard_map(
             local_block,

time: 880 us -> 848 us (0.964)
  local copies, waits for them, and re-layouts: 20.5 us -> 2.09 us
  Pallas kernels: 858 us -> 843 us
    pallas_call x1, Pallas kernels: 858 us -> 832 us  [local_block(): pl.pallas_call(functools.partial(block_kernel, cfg), out_shape=[jax.Shape...]
    unnamed x6 -> x0, local copies, waits for them, and re-layouts: 18.4 us -> none
    pallas_call x0 -> x1, Pallas kernels: none -> 11.6 us  [copy_out(): pl.pallas_call(functools.partial(copy_out_kernel, steps), out_shape=[jax....]
where the time goes in v2:
time: 848 us; the launch traced here: 847 us
  Pallas kernels  843 us (99%)
    pallas_call x1, Pallas kernels, local_block(): pl.pallas_call(functools.partial(block_kernel, cfg), out_shape=[jax.Shape...  832 us

profile of v2, /device:TPU:0, one launch (start us, length us, event | category | flops | bytes accessed | tf_op | source)
XLA Modules:
  0.0 846.6 jit_solution(10450081531636058575)
XLA Ops:
  0.6 0.7 concatenate.17
  1.3 0.7 concatenate.16
  2.0 0.7 concatenate.19
  2.7 0.6 convert_element_type.10.gains_hbm
  3.3 831.7 %mla_block.1 = (bf16[1024,7168]{1,0:T(8,128)(2,1)}, bf16[1024,512]{1,0:T(8,128)(2,1)}, bf16[2,64,512]{2,1,0:T(8,128)(2,1)}, bf16[7168,1536]{1,0:T(8,128)(2,1)}, ...) custom-call(bf16[1024,7168]{1,0:T(8,128)(2,1)} %bitcast.6, ...), custom_call_target="tpu_custom_call" | custom-call | tf_op jit(solution)/shard_map/mla_block/pallas_call | solution.py:520
  835.0 11.6 %copy_out.1 = (bf16[1024,7168]{1,0:T(8,128)(2,1)}, bf16[1024,512]{1,0:T(8,128)(2,1)}, bf16[2,64,512]{2,1,0:T(8,128)(2,1)}) custom-call(bf16[1024,7168]{1,0:T(8,128)(2,1)} %get-tuple-element.9.y_in, bf16[1024,512]{1,0:T(8,128)(2,1)} %get-tuple-element.10.c_in, bf16[2,64,512]{2,1,0:T(8,128)(2,1)} %get-tuple-element.11.r_in), custom_call_target="tpu_custom_call" | custom-call | tf_op jit(solution)/shard_map/copy_out/pallas_call | solution.py:481

commit v3 on v2

--- a/solution.py
+++ b/solution.py
@@ -19,6 +19,8 @@
 N_DEV = 8
 LOOKAHEAD = 3
 LAG = 4
+K1_VMEM = 50_600_000
+COPY_VMEM = 20_000_000
 
 
 def rope_consts(seq_len, rope_dim):
@@ -49,10 +51,10 @@
 def block_kernel(
     cfg,
     x_hbm, gains_hbm, w_dq, w_uq, w_dkv, w_ukv, w_o, cos_hbm, sin_hbm,
-    y_hbm, c_hbm, r_hbm, g_dq, g_uq, g_dkv, g_ukv, g_o,
-    ao, qd, cq, c_s, r_lo, r_hi, r_out, cos_s, sin_s, gbuf, g1row, gqrow, gkvrow,
-    wkv, wbig, wuq, wukv, q4, kv4, acc, xres, yout,
-    send_sem, recv_sem, load_sem, x_sem, y_sem, misc_sem, gain_send, gain_recv,
+    y_v, c_s, r_out, g_dq, g_uq, g_dkv, g_ukv, g_o,
+    ao, qd, cq, r_lo, r_hi, cos_s, sin_s, gbuf, g1row, gqrow, gkvrow,
+    wbig, wuq, wukv, q4, kv4, xres,
+    send_sem, recv_sem, load_sem, x_sem, misc_sem, gain_send, gain_recv,
 ):
     tok = cfg["tok"]
     seq = cfg["seq"]
@@ -82,7 +84,7 @@
     gain_copies = []
     for k in range(1, N_DEV):
         gain_copies.append(pltpu.make_async_remote_copy(
-            src_ref=gains_hbm.at[0], dst_ref=gbuf.at[me], send_sem=gain_send.at[k], recv_sem=gain_recv.at[k],
+            src_ref=gains_hbm, dst_ref=gbuf.at[me], send_sem=gain_send.at[k], recv_sem=gain_recv.at[k],
             device_id=dev(me ^ k), device_id_type=MESH))
         gain_copies[-1].start()
 
@@ -175,6 +177,8 @@
 
     def o_pieces(n):
         return [Piece(w_o, g_o, w_o.shape[0], first_u + 2 * n_u + n, n * o_w, o_w)]
+
+    wkv = y_v.at[pl.ds(0, w_dkv.shape[0]), :]
 
     def kv_bufs(_):
         return [(wkv, load_sem.at[4])]
@@ -244,16 +248,13 @@
             return carry
 
         lax.fori_loop(0, n_mb, body, 0)
-        pltpu.make_async_copy(c_s, c_hbm, misc_sem.at[0]).start()
-        pltpu.make_async_copy(r_out, r_hbm, misc_sem.at[1]).start()
 
     def compute_dq(c):
         slot = c % 2
-        cols = pl.ds(pl.multiple_of(c * dq_w, 128), dq_w)
 
         def body(m, carry):
             rows = pl.ds(pl.multiple_of(m * mb, mb), mb)
-            qd[rows, cols] = dot(ao[rows, 0:width], wbig[slot, 0:width, :])
+            qd[c, rows, :] = dot(ao[rows, 0:width], wbig[slot, 0:width, :])
             return carry
 
         lax.fori_loop(0, n_mb, body, 0)
@@ -262,9 +263,12 @@
         def _():
             def norm(m, carry):
                 rows = pl.ds(pl.multiple_of(m * 32, 32), 32)
-                v = qd[rows, :]
-                inv = lax.rsqrt(jnp.mean(v * v, axis=-1, keepdims=True) + EPSILON)
-                cq[rows, :] = (v * inv * gqrow[...]).astype(BF16)
+                vs = [qd[j, rows, :] for j in range(n_dq)]
+                mean = sum(jnp.sum(v * v, axis=-1, keepdims=True) for v in vs) * (1.0 / q_rank)
+                inv = lax.rsqrt(mean + EPSILON)
+                for j, v in enumerate(vs):
+                    cols = slice(dq_w * j, dq_w * (j + 1))
+                    cq[rows, cols] = (v * inv * gqrow[:, cols]).astype(BF16)
                 return carry
 
             lax.fori_loop(0, tok // 32, norm, 0)
@@ -333,54 +337,47 @@
 
         lax.fori_loop(0, (tok // seq) * n_pairs, attn, 0)
 
-    def y_copy(c, slot):
-        return pltpu.make_async_copy(
-            yout.at[slot], y_hbm.at[:, pl.ds(pl.multiple_of(c * o_w, 128), o_w)], y_sem.at[slot])
-
     def o_near(c, carry):
         slot = c % 2
         buf = wbig.at[slot]
         p = o_pieces(c)[0]
         p.load(buf, load_sem.at[slot], (0, 2, 4), relative=True)
         cols = pl.ds(pl.multiple_of(c * o_w, 128), o_w)
-        pltpu.make_async_copy(x_hbm.at[:, cols], xres.at[slot], x_sem.at[slot]).start()
+        pltpu.make_async_copy(x_hbm.at[:, cols], xres, x_sem).start()
         if cfg["comm"]:
             p.wait_p()
         p.load(buf, load_sem.at[slot], (1, 3, 5), relative=True)
         wait_loaded(buf.at[pl.ds(0, near), :], load_sem.at[slot])
-        wait_loaded(xres.at[slot], x_sem.at[slot])
+        wait_loaded(xres, x_sem)
 
         def body(m, carry):
             rows = pl.ds(pl.multiple_of(m * mb, mb), mb)
-            acc[c % 3, rows, :] = xres[slot, rows, :].astype(F32) + dot(ao[rows, 0:near], wbig[slot, 0:near, :])
-            return carry
-
-        lax.fori_loop(0, n_mb, body, 0)
+            qd[c % 3, rows, :] = xres[rows, :].astype(F32) + dot(ao[rows, 0:near], wbig[slot, 0:near, :])
+            return carry
+
+        if cfg["mm"]:
+            lax.fori_loop(0, n_mb, body, 0)
         return carry
 
     def o_far(c, carry):
         slot = c % 2
         buf = wbig.at[slot]
         p = o_pieces(c)[0]
+        cols = pl.ds(pl.multiple_of(c * o_w, 128), o_w)
         p.load(buf, load_sem.at[2 + slot], (6,), relative=True)
         if cfg["comm"]:
             p.wait_pd()
         p.load(buf, load_sem.at[2 + slot], (7,), relative=True)
-
-        @pl.when(c >= 2)
-        def _():
-            y_copy(c - 2, slot).wait()
-
         wait_loaded(buf.at[pl.ds(near, kdim - near), :], load_sem.at[2 + slot])
 
         def body(m, carry):
             rows = pl.ds(pl.multiple_of(m * mb, mb), mb)
-            yout[slot, rows, :] = (
-                acc[c % 3, rows, :] + dot(ao[rows, near:kdim], wbig[slot, near:kdim, :])).astype(BF16)
-            return carry
-
-        lax.fori_loop(0, n_mb, body, 0)
-        y_copy(c, slot).start()
+            y_v[rows, cols] = (
+                qd[c % 3, rows, :] + dot(ao[rows, near:kdim], wbig[slot, near:kdim, :])).astype(BF16)
+            return carry
+
+        if cfg["mm"]:
+            lax.fori_loop(0, n_mb, body, 0)
         return carry
 
     def compute(k, c):
@@ -396,7 +393,7 @@
                 send_own(k, i - first)
 
     local = [
-        pltpu.make_async_copy(gains_hbm.at[0], gbuf.at[me], misc_sem.at[2]),
+        pltpu.make_async_copy(gains_hbm, gbuf.at[me], misc_sem.at[2]),
         pltpu.make_async_copy(cos_hbm, cos_s, misc_sem.at[3]),
         pltpu.make_async_copy(sin_hbm, sin_s, misc_sem.at[4]),
         pltpu.make_async_copy(x_hbm, ao.at[:, pl.ds(0, width)], misc_sem.at[5]),
@@ -408,11 +405,14 @@
     for k in range(1, N_DEV):
         gain_copies[k - 1].wait()
 
-    n1, nq, nkv = width // N_DEV, q_rank // N_DEV, kv_rank // N_DEV
+    gq_parts, gkv_parts = [], []
     for j in range(N_DEV):
-        g1row[:, n1 * j:n1 * (j + 1)] = gbuf[j, :, 0:n1]
-    gqrow[...] = jnp.concatenate([gbuf[j, :, n1:n1 + nq] for j in range(N_DEV)], axis=1)
-    gkvrow[...] = jnp.concatenate([gbuf[j, :, n1 + nq:n1 + nq + nkv] for j in range(N_DEV)], axis=1)
+        for t in range(7):
+            g1row[:, 896 * j + 128 * t:896 * j + 128 * (t + 1)] = gbuf[j, t:t + 1, :]
+        gq_parts += [gbuf[j, 7:8, :], gbuf[j, 8:9, 0:64]]
+        gkv_parts += [gbuf[j, 8:9, 64:128]]
+    gqrow[...] = jnp.concatenate(gq_parts, axis=1)
+    gkvrow[...] = jnp.concatenate(gkv_parts, axis=1)
 
     if cfg["compute"]:
         def norm_x(m, carry):
@@ -428,7 +428,7 @@
         each_kind(i, fn, kinds[:3])
 
     def near_done(n):
-        return jnp.clip(jnp.minimum(n + 1, 2 * (n - LAG + 1)), 0, n_o)
+        return jnp.clip(jnp.minimum(n + 1, 2 * (n - LAG)), 0, n_o)
 
     def far_done(n):
         return jnp.clip(jnp.minimum(n - 1, near_done(n)), 0, n_o)
@@ -437,13 +437,15 @@
         if cfg["comm"]:
             each_kind(i, on_xy)
             each_kind(i + LA, send_own)
+        n = i - first_o
+        if cfg["compute"] and 3 not in cfg["skip"]:
+            lax.fori_loop(near_done(n - 1), near_done(n), o_near, 0)
+        if cfg["comm"]:
             each_kind(i - 2, on_d)
         each_early(i - 3, arrive)
         if cfg["compute"]:
             each_early(i - LAG, compute)
             if 3 not in cfg["skip"]:
-                n = i - first_o
-                lax.fori_loop(near_done(n - 1), near_done(n), o_near, 0)
                 lax.fori_loop(far_done(n - 1), far_done(n), o_far, 0)
         return carry
 
@@ -456,41 +458,35 @@
     if cfg["comm"]:
         lax.fori_loop(0, n_ticks, drain, 0)
     if cfg["compute"]:
-        if 0 not in cfg["skip"]: pltpu.make_async_copy(c_s, c_hbm, misc_sem.at[0]).wait()
-        if 0 not in cfg["skip"]: pltpu.make_async_copy(r_out, r_hbm, misc_sem.at[1]).wait()
-        if 3 not in cfg["skip"]: y_copy(n_o - 2, (n_o - 2) % 2).wait()
-        if 3 not in cfg["skip"]: y_copy(n_o - 1, (n_o - 1) % 2).wait()
-
-
-def copy_out_kernel(steps, y_in, c_in, r_in, y_out, c_out, r_out, y_buf, c_buf, r_buf, sem_in, sem_out):
-    n = y_in.shape[0] // steps
-    chunks = [(y_in.at[pl.ds(i * n, n)], y_buf.at[pl.ds(i * n, n)], y_out.at[pl.ds(i * n, n)]) for i in range(steps)]
-    chunks += [(c_in, c_buf, c_out), (r_in, r_buf, r_out)]
-    for i, (src, buf, _) in enumerate(chunks):
-        pltpu.make_async_copy(src, buf, sem_in.at[i]).start()
-    for i, (src, buf, dst) in enumerate(chunks):
-        pltpu.make_async_copy(src, buf, sem_in.at[i]).wait()
-        pltpu.make_async_copy(buf, dst, sem_out.at[i]).start()
-    for i, (_, buf, dst) in enumerate(chunks):
-        pltpu.make_async_copy(buf, dst, sem_out.at[i]).wait()
+        pass
+
+
+def copy_out_kernel(steps, y_v, c_v, r_v, y_out, c_out, r_out, sem):
+    n = y_v.shape[0] // steps
+    copies = [(y_v.at[pl.ds(i * n, n)], y_out.at[pl.ds(i * n, n)]) for i in range(steps)]
+    copies = [
+        pltpu.make_async_copy(src, dst, sem.at[i])
+        for i, (src, dst) in enumerate(copies + [(c_v, c_out), (r_v, r_out)])]
+    for cp in copies:
+        cp.start()
+    for cp in copies:
+        cp.wait()
 
 
 def copy_out(y, c, r):
-    steps = 16
-    any_spec = pl.BlockSpec(memory_space=pl.ANY)
+    steps = 8
     return pl.pallas_call(
         functools.partial(copy_out_kernel, steps),
         out_shape=[jax.ShapeDtypeStruct(v.shape, v.dtype) for v in (y, c, r)],
-        in_specs=[any_spec] * 3,
-        out_specs=[any_spec] * 3,
-        scratch_shapes=[pltpu.VMEM(v.shape, v.dtype) for v in (y, c, r)]
-        + [pltpu.SemaphoreType.DMA((steps + 2,)), pltpu.SemaphoreType.DMA((steps + 2,))],
-        compiler_params=pltpu.CompilerParams(vmem_limit_bytes=60_000_000),
+        in_specs=[pl.BlockSpec(memory_space=pltpu.VMEM)] * 3,
+        out_specs=[pl.BlockSpec(memory_space=pl.ANY)] * 3,
+        scratch_shapes=[pltpu.SemaphoreType.DMA((steps + 2,))],
+        compiler_params=pltpu.CompilerParams(vmem_limit_bytes=COPY_VMEM),
         name="copy_out",
     )(y, c, r)
 
 
-def solution(mesh, compute=True, comm=True, lookahead=LOOKAHEAD, skip=()):
+def solution(mesh, compute=True, comm=True, lookahead=LOOKAHEAD, skip=(), mm=True):
     batch_spec = P(("dp", "fsdp"))
     row_spec = P("fsdp")
     mat_spec = P("fsdp", None)
@@ -511,18 +507,20 @@
                 tok=tok, seq=seq, width=width, q_rank=q_rank, kv_rank=kv_rank, kdim=w_out.shape[0],
                 n_dq=q_rank // 256, n_u=n_heads // heads_per, n_o=width // 256, dq_w=256, o_w=256,
                 uq_w=heads_per * (w_uq.shape[1] // n_heads), ukv_w=heads_per * (w_ukv.shape[1] // n_heads),
-                score_scale=(w_uq.shape[1] // n_heads) ** -0.5, mb=256, compute=compute, comm=comm, lookahead=lookahead, skip=skip,
+                score_scale=(w_uq.shape[1] // n_heads) ** -0.5, mb=256, compute=compute, comm=comm, lookahead=lookahead, skip=skip, mm=mm,
             )
             n_sems = 1 + cfg["n_dq"] + 2 * cfg["n_u"] + cfg["n_o"]
-            n_g = g1.shape[0] + gq.shape[0] + gkv.shape[0]
-            gains = jnp.concatenate([g1, gq, gkv]).astype(F32).reshape(1, 1, n_g)
+            n1, nq, nkv = g1.shape[0], gq.shape[0], gkv.shape[0]
+            gains = (
+                jnp.pad(g1.astype(F32), (0, nq + nkv)) + jnp.pad(gq.astype(F32), (n1, nkv))
+                + jnp.pad(gkv.astype(F32), (n1 + nq, 0))).reshape(9, 128)
             any_spec = pl.BlockSpec(memory_space=pl.ANY)
             outs = pl.pallas_call(
                 functools.partial(block_kernel, cfg),
                 out_shape=[
-                    jax.ShapeDtypeStruct((tok, width), BF16),
-                    jax.ShapeDtypeStruct((tok, kv_rank), BF16),
-                    jax.ShapeDtypeStruct((n_prompts, rope_dim, seq), BF16),
+                    pltpu.VMEM((tok, width), BF16),
+                    pltpu.VMEM((tok, kv_rank), BF16),
+                    pltpu.VMEM((n_prompts, rope_dim, seq), BF16),
                     jax.ShapeDtypeStruct(w_dq.shape, BF16),
                     jax.ShapeDtypeStruct(w_uq.shape, BF16),
                     jax.ShapeDtypeStruct(w_dkv.shape[::-1], BF16),
@@ -530,41 +528,35 @@
                     jax.ShapeDtypeStruct(w_out.shape, BF16),
                 ],
                 in_specs=[any_spec] * 9,
-                out_specs=[any_spec] * 8,
+                out_specs=[pl.BlockSpec(memory_space=pltpu.VMEM)] * 3 + [any_spec] * 5,
                 scratch_shapes=[
                     pltpu.VMEM((tok, cfg["kdim"]), BF16),
-                    pltpu.VMEM((tok, q_rank), F32),
+                    pltpu.VMEM((cfg["n_dq"], tok, 256), F32),
                     pltpu.VMEM((tok, q_rank), BF16),
-                    pltpu.VMEM((tok, kv_rank), BF16),
                     pltpu.VMEM((tok, 128), BF16),
                     pltpu.VMEM((tok, 128), BF16),
-                    pltpu.VMEM((n_prompts, rope_dim, seq), BF16),
                     pltpu.VMEM((seq, 128), F32),
                     pltpu.VMEM((seq, 128), F32),
-                    pltpu.VMEM((N_DEV, 1, n_g), F32),
+                    pltpu.VMEM((N_DEV, 9, 128), F32),
                     pltpu.VMEM((1, width), F32),
                     pltpu.VMEM((1, q_rank), F32),
                     pltpu.VMEM((1, kv_rank), F32),
-                    pltpu.VMEM(w_dkv.shape[::-1], BF16),
                     pltpu.VMEM((2, cfg["kdim"], 256), BF16),
                     pltpu.VMEM((2, q_rank, cfg["uq_w"]), BF16),
                     pltpu.VMEM((2, kv_rank, cfg["ukv_w"]), BF16),
                     pltpu.VMEM((tok, cfg["uq_w"]), BF16),
                     pltpu.VMEM((tok, cfg["ukv_w"]), BF16),
-                    pltpu.VMEM((3, tok, 256), F32),
-                    pltpu.VMEM((2, tok, 256), BF16),
-                    pltpu.VMEM((2, tok, 256), BF16),
+                    pltpu.VMEM((tok, 256), BF16),
                     pltpu.SemaphoreType.DMA((n_sems,)),
                     pltpu.SemaphoreType.DMA((n_sems, 5)),
                     pltpu.SemaphoreType.DMA((9,)),
-                    pltpu.SemaphoreType.DMA((2,)),
-                    pltpu.SemaphoreType.DMA((2,)),
+                    pltpu.SemaphoreType.DMA,
                     pltpu.SemaphoreType.DMA((6,)),
                     pltpu.SemaphoreType.DMA((N_DEV,)),
                     pltpu.SemaphoreType.DMA((N_DEV,)),
                 ],
                 compiler_params=pltpu.CompilerParams(
-                    collective_id=0, has_side_effects=True, vmem_limit_bytes=66_000_000),
+                    collective_id=0, has_side_effects=True, vmem_limit_bytes=K1_VMEM),
                 name="mla_block",
             )(tok_blk.reshape(tok, width), gains, wdq, wuq, wdkv.T, wukv, wo, jnp.asarray(cos2), jnp.asarray(sin2))
             y, c, r = copy_out(*outs[:3])

time: 848 us -> 839 us (0.989)
  no operation moved by 1% of the time
where the time goes in v3:
time: 839 us; the launch traced here: 837 us
  Pallas kernels  835 us (100%)
    pallas_call x1, Pallas kernels, local_block(): pl.pallas_call(functools.partial(block_kernel, cfg), out_shape=[pltpu.VME...  829 us

profile of v3, /device:TPU:0, one launch (start us, length us, event | category | flops | bytes accessed | tf_op | source)
XLA Modules:
  0.0 836.6 jit_solution(15441815017324346844)
XLA Ops:
  0.6 1.4 add_bitcast_fusion.gains_hbm
  2.0 829.0 %mla_block.1 = (bf16[1024,7168]{1,0:T(8,128)(2,1)S(1)}, bf16[1024,512]{1,0:T(8,128)(2,1)S(1)}, bf16[2,64,512]{2,1,0:T(8,128)(2,1)S(1)}, bf16[7168,1536]{1,0:T(8,...) custom-call(bf16[1024,7168]{1,0:T(8,128)(2,1)} %bitcast.7, ...), custom_call_target="tpu_custom_call" | custom-call | tf_op jit(solution)/shard_map/mla_block/pallas_call | solution.py:518
  831.0 5.6 copy_out.1

commit v4 on v3

--- a/solution.py
+++ b/solution.py
@@ -19,7 +19,8 @@
 N_DEV = 8
 LOOKAHEAD = 3
 LAG = 4
-K1_VMEM = 50_600_000
+DRAIN_LAG = 6
+K1_VMEM = 51_100_000
 COPY_VMEM = 20_000_000
 
 
@@ -216,15 +217,17 @@
         for p in kinds[k][2](c):
             p.on_d()
 
+    def drain(k, c):
+        for p in kinds[k][2](c):
+            p.drain()
+
     def arrive(k, c):
         ps = kinds[k][2](c)
-        if cfg["comm"]:
-            for p in ps:
-                p.wait_p()
-                p.wait_pd()
-        if cfg["compute"]:
-            for p, (buf, sem) in zip(ps, kinds[k][3](c)):
-                p.load(buf, sem, range(N_DEV))
+        for p in ps:
+            p.wait_p()
+            p.wait_pd()
+        for p, (buf, sem) in zip(ps, kinds[k][3](c)):
+            p.load(buf, sem, range(N_DEV))
 
     mb = cfg["mb"]
     n_mb = tok // mb
@@ -337,57 +340,61 @@
 
         lax.fori_loop(0, (tok // seq) * n_pairs, attn, 0)
 
-    def o_near(c, carry):
+    def near_rows(slot):
+        return wbig.at[slot].at[pl.ds(0, near), :]
+
+    def far_rows(slot):
+        return wbig.at[slot].at[pl.ds(near, kdim - near), :]
+
+    def near_load(c, carry):
         slot = c % 2
-        buf = wbig.at[slot]
         p = o_pieces(c)[0]
-        p.load(buf, load_sem.at[slot], (0, 2, 4), relative=True)
-        cols = pl.ds(pl.multiple_of(c * o_w, 128), o_w)
-        pltpu.make_async_copy(x_hbm.at[:, cols], xres, x_sem).start()
-        if cfg["comm"]:
-            p.wait_p()
-        p.load(buf, load_sem.at[slot], (1, 3, 5), relative=True)
-        wait_loaded(buf.at[pl.ds(0, near), :], load_sem.at[slot])
-        wait_loaded(xres, x_sem)
+        p.load(wbig.at[slot], load_sem.at[slot], (0, 2, 4), relative=True)
+        pltpu.make_async_copy(
+            x_hbm.at[:, pl.ds(pl.multiple_of(c * o_w, 128), o_w)], xres.at[slot], x_sem.at[slot]).start()
+        p.wait_p()
+        p.load(wbig.at[slot], load_sem.at[slot], (1, 3, 5), relative=True)
+        return carry
+
+    def near_sum(c, carry):
+        slot = c % 2
+        wait_loaded(near_rows(slot), load_sem.at[slot])
+        wait_loaded(xres.at[slot], x_sem.at[slot])
 
         def body(m, carry):
             rows = pl.ds(pl.multiple_of(m * mb, mb), mb)
-            qd[c % 3, rows, :] = xres[rows, :].astype(F32) + dot(ao[rows, 0:near], wbig[slot, 0:near, :])
+            qd[c % n_dq, rows, :] = xres[slot, rows, :].astype(F32) + dot(ao[rows, 0:near], wbig[slot, 0:near, :])
             return carry
 
-        if cfg["mm"]:
-            lax.fori_loop(0, n_mb, body, 0)
+        return lax.fori_loop(0, n_mb, body, carry)
+
+    def far_load(c, carry):
+        slot = c % 2
+        p = o_pieces(c)[0]
+        p.load(wbig.at[slot], load_sem.at[2 + slot], (6,), relative=True)
+        p.wait_pd()
+        p.load(wbig.at[slot], load_sem.at[2 + slot], (7,), relative=True)
         return carry
 
-    def o_far(c, carry):
+    def far_sum(c, carry):
         slot = c % 2
-        buf = wbig.at[slot]
-        p = o_pieces(c)[0]
         cols = pl.ds(pl.multiple_of(c * o_w, 128), o_w)
-        p.load(buf, load_sem.at[2 + slot], (6,), relative=True)
-        if cfg["comm"]:
-            p.wait_pd()
-        p.load(buf, load_sem.at[2 + slot], (7,), relative=True)
-        wait_loaded(buf.at[pl.ds(near, kdim - near), :], load_sem.at[2 + slot])
+        wait_loaded(far_rows(slot), load_sem.at[2 + slot])
 
         def body(m, carry):
             rows = pl.ds(pl.multiple_of(m * mb, mb), mb)
             y_v[rows, cols] = (
-                qd[c % 3, rows, :] + dot(ao[rows, near:kdim], wbig[slot, near:kdim, :])).astype(BF16)
+                qd[c % n_dq, rows, :] + dot(ao[rows, near:kdim], wbig[slot, near:kdim, :])).astype(BF16)
             return carry
 
-        if cfg["mm"]:
-            lax.fori_loop(0, n_mb, body, 0)
-        return carry
+        return lax.fori_loop(0, n_mb, body, carry)
 
     def compute(k, c):
         for (buf, sem) in kinds[k][3](c):
             wait_loaded(buf.at[pl.ds(0, width), :] if k == 1 else buf, sem)
-        if k not in cfg["skip"]:
-            (compute_kv, compute_dq, compute_u)[k](c)
-
-    LA = cfg["lookahead"]
-    for i in range(LA if cfg["comm"] else 0):
+        (compute_kv, compute_dq, compute_u)[k](c)
+
+    for i in range(LOOKAHEAD):
         for k, (first, count, _, _) in enumerate(kinds):
             if first <= i < first + count:
                 send_own(k, i - first)
@@ -414,15 +421,14 @@
     gqrow[...] = jnp.concatenate(gq_parts, axis=1)
     gkvrow[...] = jnp.concatenate(gkv_parts, axis=1)
 
-    if cfg["compute"]:
-        def norm_x(m, carry):
-            rows = pl.ds(pl.multiple_of(m * 16, 16), 16)
-            v = ao[rows, 0:width].astype(F32)
-            inv = lax.rsqrt(jnp.mean(v * v, axis=-1, keepdims=True) + EPSILON)
-            ao[rows, 0:width] = (v * inv * g1row[...]).astype(BF16)
-            return carry
-
-        lax.fori_loop(0, tok // 16, norm_x, 0)
+    def norm_x(m, carry):
+        rows = pl.ds(pl.multiple_of(m * 16, 16), 16)
+        v = ao[rows, 0:width].astype(F32)
+        inv = lax.rsqrt(jnp.mean(v * v, axis=-1, keepdims=True) + EPSILON)
+        ao[rows, 0:width] = (v * inv * g1row[...]).astype(BF16)
+        return carry
+
+    lax.fori_loop(0, tok // 16, norm_x, 0)
 
     def each_early(i, fn):
         each_kind(i, fn, kinds[:3])
@@ -434,31 +440,26 @@
         return jnp.clip(jnp.minimum(n - 1, near_done(n)), 0, n_o)
 
     def tick(i, carry):
-        if cfg["comm"]:
-            each_kind(i, on_xy)
-            each_kind(i + LA, send_own)
+        each_kind(i, on_xy)
+        each_kind(i + LOOKAHEAD, send_own)
         n = i - first_o
-        if cfg["compute"] and 3 not in cfg["skip"]:
-            lax.fori_loop(near_done(n - 1), near_done(n), o_near, 0)
-        if cfg["comm"]:
-            each_kind(i - 2, on_d)
+        for fn in (near_load, near_sum):
+            lax.fori_loop(near_done(n - 1), near_done(n), fn, 0)
+        each_kind(i - 2, on_d)
+        lax.fori_loop(far_done(n - 2), far_done(n - 1), far_sum, 0)
+        lax.fori_loop(far_done(n - 1), far_done(n), far_load, 0)
+        each_kind(i - DRAIN_LAG, drain)
         each_early(i - 3, arrive)
-        if cfg["compute"]:
-            each_early(i - LAG, compute)
-            if 3 not in cfg["skip"]:
-                lax.fori_loop(far_done(n - 1), far_done(n), o_far, 0)
+        each_early(i - LAG, compute)
         return carry
 
-    lax.fori_loop(0, n_ticks + 2, tick, 0)
-
-    def drain(i, carry):
-        each_kind(i, lambda k, c: [p.drain() for p in kinds[k][2](c)])
+    lax.fori_loop(0, n_ticks + 3, tick, 0)
+
+    def finish(i, carry):
+        each_kind(i, drain)
         return carry
 
-    if cfg["comm"]:
-        lax.fori_loop(0, n_ticks, drain, 0)
-    if cfg["compute"]:
-        pass
+    lax.fori_loop(n_ticks + 3 - DRAIN_LAG, n_ticks, finish, 0)
 
 
 def copy_out_kernel(steps, y_v, c_v, r_v, y_out, c_out, r_out, sem):
@@ -486,7 +487,7 @@
     )(y, c, r)
 
 
-def solution(mesh, compute=True, comm=True, lookahead=LOOKAHEAD, skip=(), mm=True):
+def solution(mesh):
     batch_spec = P(("dp", "fsdp"))
     row_spec = P("fsdp")
     mat_spec = P("fsdp", None)
@@ -507,7 +508,7 @@
                 tok=tok, seq=seq, width=width, q_rank=q_rank, kv_rank=kv_rank, kdim=w_out.shape[0],
                 n_dq=q_rank // 256, n_u=n_heads // heads_per, n_o=width // 256, dq_w=256, o_w=256,
                 uq_w=heads_per * (w_uq.shape[1] // n_heads), ukv_w=heads_per * (w_ukv.shape[1] // n_heads),
-                score_scale=(w_uq.shape[1] // n_heads) ** -0.5, mb=256, compute=compute, comm=comm, lookahead=lookahead, skip=skip, mm=mm,
+                score_scale=(w_uq.shape[1] // n_heads) ** -0.5, mb=256,
             )
             n_sems = 1 + cfg["n_dq"] + 2 * cfg["n_u"] + cfg["n_o"]
             n1, nq, nkv = g1.shape[0], gq.shape[0], gkv.shape[0]
@@ -546,11 +547,11 @@
                     pltpu.VMEM((2, kv_rank, cfg["ukv_w"]), BF16),
                     pltpu.VMEM((tok, cfg["uq_w"]), BF16),
                     pltpu.VMEM((tok, cfg["ukv_w"]), BF16),
-                    pltpu.VMEM((tok, 256), BF16),
+                    pltpu.VMEM((2, tok, 256), BF16),
                     pltpu.SemaphoreType.DMA((n_sems,)),
                     pltpu.SemaphoreType.DMA((n_sems, 5)),
                     pltpu.SemaphoreType.DMA((9,)),
-                    pltpu.SemaphoreType.DMA,
+                    pltpu.SemaphoreType.DMA((2,)),
                     pltpu.SemaphoreType.DMA((6,)),
                     pltpu.SemaphoreType.DMA((N_DEV,)),
                     pltpu.SemaphoreType.DMA((N_DEV,)),

time: 839 us -> 836 us (level)
  no operation moved by 1% of the time
where the time goes in v4:
time: 836 us; the launch traced here: 835 us
  Pallas kernels  833 us (100%)
    pallas_call x1, Pallas kernels, local_block(): pl.pallas_call(functools.partial(block_kernel, cfg), out_shape=[pltpu.VME...  828 us

profile of v4, /device:TPU:0, one launch (start us, length us, event | category | flops | bytes accessed | tf_op | source)
XLA Modules:
  0.0 835.4 jit_solution(7380664413667066463)
XLA Ops:
  0.6 1.4 add_bitcast_fusion.gains_hbm
  2.0 827.8 %mla_block.1 = (bf16[1024,7168]{1,0:T(8,128)(2,1)S(1)}, bf16[1024,512]{1,0:T(8,128)(2,1)S(1)}, bf16[2,64,512]{2,1,0:T(8,128)(2,1)S(1)}, bf16[7168,1536]{1,0:T(8,...) custom-call(bf16[1024,7168]{1,0:T(8,128)(2,1)} %bitcast.7, ...), custom_call_target="tpu_custom_call" | custom-call | tf_op jit(solution)/shard_map/mla_block/pallas_call | solution.py:519
  829.8 5.6 copy_out.1
